TPU v7x, 8 devices: a whole 2x2x1 slice. The times are simulated.
8 devices in a mesh: dp: 1 (over z), ep: 8 (over y, x, core).
Axes of the slice: x: 2, y: 2, z: 1, core: 2. Of those that a mesh axis runs over, the one named last changes fastest.
Arguments:
- tokens: bfloat16 [8, 512, 2048], P(('dp', 'ep'))
- w_query: bfloat16 [2048, 32, 128], P('ep')
- w_key: bfloat16 [2048, 32, 128], P('ep')
- w_value: bfloat16 [2048, 32, 128], P('ep')
- w_out: bfloat16 [4096, 2048], P('ep')
- w_router: float32 [2048, 128], replicated
- w_one: bfloat16 [128, 2048, 768], P('ep')
- w_three: bfloat16 [128, 2048, 768], P('ep')
- w_two: bfloat16 [128, 768, 2048], P('ep')
- expert_ids: int32 [8, 512, 8], P(('dp', 'ep'))
Outputs:
- output: bfloat16 [8, 512, 2048], P(('dp', 'ep'))
All inputs are finite; a program needn't handle non-finite values.
Results may differ from a plain program's by a relative error of at most 0.00978195.
Values are sent between devices in bfloat16 or wider.
A program may use at most 1 GiB of HBM per device.

v0:
```python
import jax
import jax.numpy as jnp
from jax import lax
from jax.sharding import PartitionSpec as P

EPS = 1e-6


def rms_norm(vals):
    wide = vals.astype(jnp.float32)
    return wide * lax.rsqrt(jnp.mean(wide * wide, axis=-1, keepdims=True) + EPS)


def attention_layer(tokens, w_query, w_key, w_value, w_out):
    seq_count = tokens.shape[0]
    seq_len = tokens.shape[1]
    head_dim = w_query.shape[2]
    normed = rms_norm(tokens).astype(jnp.bfloat16)
    query = jnp.einsum('bsd,dhk->bshk', normed, w_query, preferred_element_type=jnp.float32).astype(jnp.bfloat16)
    keys = jnp.einsum('bsd,dhk->bshk', normed, w_key, preferred_element_type=jnp.float32).astype(jnp.bfloat16)
    values = jnp.einsum('bsd,dhk->bshk', normed, w_value, preferred_element_type=jnp.float32).astype(jnp.bfloat16)
    scores = jnp.einsum('bqhk,bshk->bhqs', query, keys, preferred_element_type=jnp.float32) * head_dim ** -0.5
    causal = lax.broadcasted_iota(jnp.int32, (seq_len, seq_len), 0) >= lax.broadcasted_iota(jnp.int32, (seq_len, seq_len), 1)
    attn_weights = jax.nn.softmax(jnp.where(causal, scores, -jnp.inf), axis=-1).astype(jnp.bfloat16)
    context = jnp.einsum('bhqs,bshk->bqhk', attn_weights, values, preferred_element_type=jnp.float32).astype(jnp.bfloat16)
    attn_out = jnp.einsum('crd,de->cre', context.reshape(seq_count, seq_len, -1), w_out, preferred_element_type=jnp.float32)
    return (tokens.astype(jnp.float32) + attn_out).astype(jnp.bfloat16)


def router_gates(hidden, w_router, expert_ids):
    normed = rms_norm(hidden)
    logits = jnp.einsum('bsd,de->bse', normed, w_router, precision=lax.Precision.HIGHEST, preferred_element_type=jnp.float32)
    chosen = jnp.take_along_axis(logits, expert_ids, axis=-1)
    return normed.astype(jnp.bfloat16), jax.nn.softmax(chosen, axis=-1)


def dispatch_tables(ids_flat, experts, cap_rows):
    member = jnp.sum((ids_flat[:, :, None] == jnp.arange(experts, dtype=jnp.int32)).astype(jnp.int32), axis=1)
    before = jnp.cumsum(member, axis=0) - member
    slot = jnp.take_along_axis(before, ids_flat, axis=1)
    onehot = (member[:, :, None] > 0) & (before[:, :, None] == jnp.arange(cap_rows, dtype=jnp.int32))
    return onehot.astype(jnp.bfloat16), ids_flat * cap_rows + slot


def expert_ffn(rows, w_one, w_three, w_two):
    first = jnp.einsum('end,edf->enf', rows, w_one, preferred_element_type=jnp.float32)
    third = jnp.einsum('end,edf->enf', rows, w_three, preferred_element_type=jnp.float32)
    activated = (jax.nn.silu(first) * third).astype(jnp.bfloat16)
    return jnp.einsum('enf,efd->end', activated, w_two, preferred_element_type=jnp.float32).astype(jnp.bfloat16)


def combine_rows(hidden_flat, back_rows, flat_slot, gates_flat):
    table = back_rows.reshape(-1, back_rows.shape[-1])
    picked = jnp.take(table, flat_slot, axis=0)
    mixed = jnp.sum(gates_flat[:, :, None] * picked.astype(jnp.float32), axis=1)
    return (hidden_flat.astype(jnp.float32) + mixed).astype(jnp.bfloat16)


def solution(mesh):
    tok_spec = P(('dp', 'ep'))
    row_spec = P('ep')

    def local_layer(tokens, w_query, w_key, w_value, w_out, w_router, w_one, w_three, w_two, expert_ids):
        full_query = lax.all_gather(w_query, 'ep', axis=0, tiled=True)
        full_key = lax.all_gather(w_key, 'ep', axis=0, tiled=True)
        full_value = lax.all_gather(w_value, 'ep', axis=0, tiled=True)
        full_out = lax.all_gather(w_out, 'ep', axis=0, tiled=True)
        hidden = attention_layer(tokens, full_query, full_key, full_value, full_out)
        normed, gates = router_gates(hidden, w_router, expert_ids)
        seq_count, seq_len, model_dim = tokens.shape
        choices = expert_ids.shape[2]
        experts = w_router.shape[1]
        tok_count = seq_count * seq_len
        cap_rows = 2 * tok_count * choices // experts
        onehot, flat_slot = dispatch_tables(expert_ids.reshape(tok_count, choices), experts, cap_rows)
        send_rows = jnp.einsum('tec,td->ecd', onehot, normed.reshape(tok_count, model_dim), preferred_element_type=jnp.float32).astype(jnp.bfloat16)
        recv_rows = lax.all_to_all(send_rows, 'ep', 0, 1, tiled=True)
        done_rows = expert_ffn(recv_rows, w_one, w_three, w_two)
        back_rows = lax.all_to_all(done_rows, 'ep', 1, 0, tiled=True)
        layer_out = combine_rows(hidden.reshape(tok_count, model_dim), back_rows, flat_slot, gates.reshape(tok_count, choices))
        return layer_out.reshape(seq_count, seq_len, model_dim)

    return jax.shard_map(local_layer, mesh=mesh, in_specs=(tok_spec, row_spec, row_spec, row_spec, row_spec, P(), row_spec, row_spec, row_spec, tok_spec), out_specs=tok_spec, check_vma=False)
```

profile of v0, /device:TPU:0, one launch (start us, length us, event | category | flops | bytes accessed | tf_op | source)
XLA Modules:
  0.0 1498.8 jit_solution(10670823427215100193)
XLA Ops:
  10.2 3.8 convert_reduce_fusion
  17.4 1.8 copy.83
  20.7 1.1 bitcast_subtract_fusion
  21.8 74.3 %all-gather.7.cloned.1.call-done = bf16[2048,32,128]{2,1,0:T(8,128)(2,1)} async-done(((bf16[256,32,128]{2,1,0:T(8,128)(2,1)}), bf16[2048,32,128]{2,1,0:T(8,128)(2,1)}) %all-gather.7.cloned.1.call-update) | async-done | bytes 16777232 | tf_op jit(solution)/shard_map/all_gather | solution.py:64
  96.1 13.9 fusion.4
  110.0 72.0 %all-gather.9.cloned.1.call-done = bf16[2048,32,128]{2,1,0:T(8,128)(2,1)} async-done(((bf16[256,32,128]{2,1,0:T(8,128)(2,1)}), bf16[2048,32,128]{2,1,0:T(8,128)(2,1)}) %all-gather.9.cloned.1.call-update) | async-done | bytes 16777232 | tf_op jit(solution)/shard_map/all_gather | solution.py:65
  182.0 22.9 %fusion.28 = f32[32,512,512]{1,2,0:T(8,128)} fusion(bf16[2048,32,128]{2,1,0:T(8,128)(2,1)} %all-gather.9.cloned.1.call-done, bf16[512,32,128]{2,0,1:T(8,128)(2,1)} %fusion.4, bf16[1,512,2048]{2,1,0:T(8,128)(2,1)S(1)} %copy-done.5, f32[512]{0:T(512)S(1)} %add_rsqrt_fusion.1), kind=kOutput, calls=%fused_computation.43 | convolution fusion | flops 10742661120 | bytes 56625152 | tf_op jit(solution)/shard_map/bqhk,bshk->bhqs/dot_general | solution.py:22
  204.9 45.7 %fusion.63 = (f32[32,512]{1,0:T(8,128)}, f32[32,512,512]{1,2,0:T(8,128)}) fusion(f32[32,512,512]{1,2,0:T(8,128)} %fusion.28, pred[512,512]{0,1:T(8,128)(4,1)} %iota_compare_fusion.2), kind=kOutput, calls=%fused_computation.83 | output fusion | flops 50332160 | bytes 67436544 | tf_op jit(solution)/shard_map/sub | solution.py:24
  250.5 17.4 %all-gather.5.cloned.1.call-done = bf16[2048,32,128]{2,1,0:T(8,128)(2,1)} async-done(((bf16[256,32,128]{2,1,0:T(8,128)(2,1)}), bf16[2048,32,128]{2,1,0:T(8,128)(2,1)}) %all-gather.5.cloned.1.call-update) | async-done | bytes 16777232 | tf_op jit(solution)/shard_map/all_gather | solution.py:66
  267.9 21.0 %fusion.40 = bf16[32,128,512]{2,1,0:T(8,128)(2,1)} fusion(f32[32,512,512]{1,2,0:T(8,128)} %get-tuple-element.8, f32[32,512]{1,0:T(8,128)} %get-tuple-element.7, bf16[2048,32,128]{2,1,0:T(8,128)(2,1)} %all-gather.5.cloned.1.call-done, bf16[1,512,2048]{2,1,0:T(8,128)(2,1)S(1)} %copy-done.5, f32[512]{0:T(512)S(1)} %add_rsqrt_fusion.1), kind=kOutput, calls=%fused_computation.47 | convolution fusion | flops 10761535488 | bytes 56690688 | tf_op jit(solution)/shard_map/bhqs,bshk->bqhk/dot_general | solution.py:25
  289.0 64.7 %all-gather.11.cloned.1.call-done = bf16[4096,2048]{1,0:T(8,128)(2,1)} async-done(((bf16[512,2048]{1,0:T(8,128)(2,1)}), bf16[4096,2048]{1,0:T(8,128)(2,1)}) %all-gather.11.cloned.1.call-update) | async-done | bytes 16777232 | tf_op jit(solution)/shard_map/all_gather | solution.py:67
  353.7 13.9 fusion.26
  367.6 1.3 copy-done.3
  368.9 21.8 %convolution_convert_fusion.1 = bf16[128,64,2048]{2,0,1:T(8,128)(2,1)} fusion(s32[512,128]{0,1:T(8,128)S(1)} %bitcast_subtract_fusion, pred[512,128]{0,1:T(8,128)(4,1)S(1)} %copy.88, bf16[1,512,2048]{2,1,0:T(8,128)(2,1)S(1)} %get-tuple-element.10, f32[512]{0:T(512)S(1)} %add_rsqrt_fusion), kind=kOutput, calls=%fused_computation.11 | convolution fusion | flops 17208180736 | bytes 35981312 | tf_op jit(solution)/shard_map/tec,td->ecd/dot_general | solution.py:76
  390.7 30.0 %copy.89 = bf16[128,64,2048]{2,1,0:T(8,128)(2,1)} copy(bf16[128,64,2048]{2,0,1:T(8,128)(2,1)} %convolution_convert_fusion.1) | data formatting | bytes 67108864 | tf_op jit(solution)/shard_map/convert_element_type | solution.py:76
  420.7 373.6 %all_to_all.33 = bf16[128,64,2048]{2,1,0:T(8,128)(2,1)} all-to-all(bf16[128,64,2048]{2,1,0:T(8,128)(2,1)} %copy.89), channel_id=1, replica_groups=mesh['dp'=1,'ep'=8] {'ep'}, dimensions={0} | all-to-all | bytes 67108864 | tf_op jit(solution)/shard_map/all_to_all | solution.py:77
  794.3 22.9 %copy.90 = bf16[8,16,64,2048]{3,2,0,1:T(8,128)(2,1)} copy(bf16[8,16,64,2048]{3,2,1,0:T(8,128)(2,1)} %bitcast.88) | data formatting | bytes 67108864 | tf_op jit(solution)/shard_map/all_to_all | solution.py:77
  817.2 41.0 %fusion.64 = f32[16,512,768]{2,1,0:T(8,128)} fusion(bf16[16,512,2048]{2,1,0:T(8,128)(2,1)} %bitcast.89, bf16[16,2048,768]{2,1,0:T(8,128)(2,1)} %param.16), kind=kOutput, calls=%fused_computation.84 | convolution fusion | flops 25769803776 | bytes 109051904 | tf_op jit(solution)/shard_map/end,edf->enf/dot_general | solution.py:46
  858.2 49.2 %multiply_convert_fusion.4 = bf16[16,512,768]{2,1,0:T(8,128)(2,1)} fusion(f32[16,512,768]{2,1,0:T(8,128)} %fusion.64, bf16[16,512,2048]{2,1,0:T(8,128)(2,1)} %bitcast.90, bf16[16,2048,768]{2,1,0:T(8,128)(2,1)} %param.17), kind=kOutput, calls=%fused_computation.9.clone.clone.1 | convolution fusion | flops 25807552512 | bytes 121634816 | tf_op jit(solution)/shard_map/end,edf->enf/dot_general | solution.py:47
  907.5 39.0 %convolution_convert_fusion = bf16[16,512,2048]{2,1,0:T(8,128)(2,1)} fusion(bf16[16,768,2048]{2,1,0:T(8,128)(2,1)} %param.18, bf16[16,512,768]{2,1,0:T(8,128)(2,1)} %multiply_convert_fusion.4), kind=kOutput, calls=%fused_computation.10 | convolution fusion | flops 25786580992 | bytes 96468992 | tf_op jit(solution)/shard_map/enf,efd->end/dot_general | solution.py:49
  946.5 30.0 %copy.91 = bf16[16,512,2048]{2,0,1:T(8,128)(2,1)} copy(bf16[16,512,2048]{2,1,0:T(8,128)(2,1)} %convolution_convert_fusion) | data formatting | bytes 67108864 | tf_op jit(solution)/shard_map/convert_element_type | solution.py:49
  976.5 6.1 all-to-all-start.1
  983.6 33.0 %gather_fusion.2 = s32[4096]{0:T(1024)S(1)} fusion(s32[512,128]{0,1:T(8,128)S(1)} %copy-done.2, s32[4096]{0:T(1024)S(1)} %reshape.270), kind=kCustom, calls=%fused_computation.2 | custom fusion | bytes 65536 | tf_op jit(solution)/shard_map/jit(take_along_axis)/gather | solution.py:40
  1019.5 1.1 reshape.256
  1021.4 1.1 reshape.264
  1022.9 4.2 fusion.21
  1027.0 25.6 %gather_fusion.1 = f32[4096]{0:T(1024)S(1)} fusion(f32[512,128]{1,0:T(8,128)S(1)} %fusion.21, s32[4096]{0:T(1024)S(1)} %reshape.264), kind=kCustom, calls=%fused_computation.1 | custom fusion | bytes 65536 | tf_op jit(solution)/shard_map/jit(take_along_axis)/gather | solution.py:33
  1053.1 293.4 %all-to-all-done.1 = bf16[16,512,2048]{2,0,1:T(8,128)(2,1)} async-done(((bf16[16,512,2048]{2,0,1:T(8,128)(2,1)}), bf16[16,512,2048]{2,0,1:T(8,128)(2,1)}, u32[]{:S(2)}, u32[]{:S(2)}) %all-to-all-start.1) | async-done | bytes 33554464 | tf_op jit(solution)/shard_map/all_to_all | solution.py:79
  1346.5 30.0 %copy.92 = bf16[16,8,64,2048]{3,2,0,1:T(8,128)(2,1)} copy(bf16[16,8,64,2048]{3,0,2,1:T(8,128)(2,1)} %bitcast.22) | data formatting | bytes 67108864 | tf_op jit(solution)/shard_map/all_to_all | solution.py:79
  1376.6 95.9 %gather_fusion = bf16[4096,2048]{1,0:T(8,128)(2,1)} fusion(bf16[8192,2048]{1,0:T(8,128)(2,1)} %bitcast.87, s32[4096]{0:T(1024)S(1)} %broadcast_clamp_fusion), kind=kCustom, calls=%fused_computation | custom fusion | bytes 33570816 | tf_op jit(solution)/shard_map/jit(_take)/gather | solution.py:54
  1472.4 17.6 %multiply_reduce_fusion = f32[512,2048]{1,0:T(8,128)S(1)} fusion(bf16[4096,2048]{1,0:T(8,128)(2,1)} %gather_fusion, f32[512,8]{1,0:T(8,128)S(1)} %copy.79, pred[512,8]{1,0:T(8,128)(4,1)S(1)} %copy.87), kind=kLoop, calls=%fused_computation.4 | loop fusion | flops 32505856 | bytes 20992000 | tf_op jit(solution)/shard_map/reduce_sum | solution.py:55
  1490.0 2.1 fusion.27
  (61 shorter events, 13.9 us)
Async XLA Ops:
  6.5 1016.3 %copy-start = (f32[2048,128]{1,0:T(8,128)S(1)}, f32[2048,128]{1,0:T(8,128)}, u32[]{:S(2)}) copy-start(f32[2048,128]{1,0:T(8,128)} %param.15) | copy-start | bytes 3145732
  6.5 2.8 copy-start.7
  6.5 13.6 copy-start.5
  6.5 89.6 %all-gather.7.cloned.1.call-start = ((), (), s32[]{:S(2)}) async-start(), calls=%async_computation.3 | async-start | bytes 18874368 | tf_op jit(solution)/shard_map/all_gather | solution.py:64
  7.3 174.8 %all-gather.9.cloned.1.call-start = ((), (), s32[]{:S(2)}) async-start(), calls=%async_computation.4 | async-start | bytes 18874368 | tf_op jit(solution)/shard_map/all_gather | solution.py:65
  8.0 259.9 %all-gather.5.cloned.1.call-start = ((), (), s32[]{:S(2)}) async-start(), calls=%async_computation.2 | async-start | bytes 18874368 | tf_op jit(solution)/shard_map/all_gather | solution.py:66
  8.7 345.0 %all-gather.11.cloned.1.call-start = ((), (), s32[]{:S(2)}) async-start(), calls=%async_computation.5 | async-start | bytes 18874368 | tf_op jit(solution)/shard_map/all_gather | solution.py:67
  15.0 0.7 copy-start.6
  21.7 345.9 %copy-start.1 = (s32[512,128]{0,1:T(8,128)}, s32[512,128]{0,1:T(8,128)S(1)}, u32[]{:S(2)}) copy-start(s32[512,128]{0,1:T(8,128)S(1)} %bitcast_subtract_fusion) | copy-start | bytes 786436
  367.6 1.3 copy-start.3
  367.6 23.1 %copy-start.9 = (f32[512]{0:T(512)}, f32[512]{0:T(512)S(1)}, u32[]{:S(2)}) copy-start(f32[512]{0:T(512)S(1)} %add_rsqrt_fusion) | copy-start | bytes 6148
  976.5 6.1 copy-start.8
  976.5 370.0 %all-to-all-start.1 = ((bf16[16,512,2048]{2,0,1:T(8,128)(2,1)}), bf16[16,512,2048]{2,0,1:T(8,128)(2,1)}, u32[]{:S(2)}, u32[]{:S(2)}) async-start(bf16[16,512,2048]{2,0,1:T(8,128)(2,1)} %copy.91), calls=%async_computation.1 | async-start | bytes 67108864 | tf_op jit(solution)/shard_map/all_to_all | solution.py:79
  982.6 1.0 copy-start.2
  983.6 39.3 %copy-start.4 = (bf16[1,512,2048]{2,1,0:T(8,128)(2,1)S(1)}, bf16[1,512,2048]{2,1,0:T(8,128)(2,1)}, u32[]{:S(2)}) copy-start(bf16[1,512,2048]{2,1,0:T(8,128)(2,1)} %copy-done.3) | copy-start | bytes 6291460
Sparse Core Ops, SparseCore 0:
  9.2 86.8 all-gather.6
  97.9 84.0 all-gather.8
  183.8 84.0 all-gather.4
  269.6 84.0 all-gather.10
where the time goes:
time: 1510 us; the launch traced here: 1500 us
  waiting for transfers between devices  525 us (35%)
  blocking collectives  374 us (25%)
  local copies, waits for them, and re-layouts  281 us (19%)
  matrix products  227 us (15%)
  other arithmetic  72.8 us (5%)
    all_to_all x1, blocking collectives, local_layer(): recv_rows = lax.all_to_all(send_rows, 'ep', 0, 1, tiled=True)  374 us
    all_to_all x1, waiting for transfers between devices, local_layer(): back_rows = lax.all_to_all(done_rows, 'ep', 1, 0, tiled=True)  293 us
    gather x1, local copies, waits for them, and re-layouts, combine_rows(): picked = jnp.take(table, flat_slot, axis=0)  95.9 us
    all_gather x1, waiting for transfers between devices, local_layer(): full_query = lax.all_gather(w_query, 'ep', axis=0, tiled=True)  74.3 us
    all_gather x1, waiting for transfers between devices, local_layer(): full_key = lax.all_gather(w_key, 'ep', axis=0, tiled=True)  72 us
    all_gather x1, waiting for transfers between devices, local_layer(): full_out = lax.all_gather(w_out, 'ep', axis=0, tiled=True)  64.7 us
    dot_general x1, matrix products, expert_ffn(): jnp.einsum('end,edf->enf', rows, w_three, preferred_element_type=jnp.floa...  49.2 us
    sub x1, other arithmetic, attention_layer(): jax.nn.softmax(jnp.where(causal, scores, -jnp.inf), axis=-1)  45.7 us
  transfers between devices with their start and end apart: 5, of which 5 were waited for; matrix products, arithmetic and copies ran while one was open for 12% of the time, Pallas kernels for 0%

commit v1 on v0

v1 whole, which is shorter than its diff:
```python
import jax
import jax.numpy as jnp
from jax import lax
from jax.sharding import PartitionSpec as P

EPS = 1e-6


def rms_norm(vals):
    wide = vals.astype(jnp.float32)
    return wide * lax.rsqrt(jnp.mean(wide * wide, axis=-1, keepdims=True) + EPS)


def attention_layer(tokens, w_query, w_key, w_value, w_out):
    seq_count = tokens.shape[0]
    seq_len = tokens.shape[1]
    head_dim = w_query.shape[2]
    normed = rms_norm(tokens).astype(jnp.bfloat16)
    query = jnp.einsum('bsd,dhk->bshk', normed, w_query, preferred_element_type=jnp.float32).astype(jnp.bfloat16)
    keys = jnp.einsum('bsd,dhk->bshk', normed, w_key, preferred_element_type=jnp.float32).astype(jnp.bfloat16)
    values = jnp.einsum('bsd,dhk->bshk', normed, w_value, preferred_element_type=jnp.float32).astype(jnp.bfloat16)
    scores = jnp.einsum('bqhk,bshk->bhqs', query, keys, preferred_element_type=jnp.float32) * head_dim ** -0.5
    causal = lax.broadcasted_iota(jnp.int32, (seq_len, seq_len), 0) >= lax.broadcasted_iota(jnp.int32, (seq_len, seq_len), 1)
    attn_weights = jax.nn.softmax(jnp.where(causal, scores, -jnp.inf), axis=-1).astype(jnp.bfloat16)
    context = jnp.einsum('bhqs,bshk->bqhk', attn_weights, values, preferred_element_type=jnp.float32).astype(jnp.bfloat16)
    attn_out = jnp.einsum('crd,de->cre', context.reshape(seq_count, seq_len, -1), w_out, preferred_element_type=jnp.float32)
    return (tokens.astype(jnp.float32) + attn_out).astype(jnp.bfloat16)


def router_gates(hidden, w_router, ids):
    normed = rms_norm(hidden)
    logits = jnp.einsum('td,de->te', normed, w_router, precision=lax.Precision.HIGHEST, preferred_element_type=jnp.float32)
    hit = ids[:, :, None] == jnp.arange(w_router.shape[1], dtype=jnp.int32)
    chosen = jnp.sum(jnp.where(hit, logits[:, None, :], 0.0), axis=2)
    return normed.astype(jnp.bfloat16), jax.nn.softmax(chosen, axis=-1)


def local_tables(all_ids, all_gates, first, count):
    wanted = first + jnp.arange(count, dtype=jnp.int32)
    hit = all_ids[:, :, :, None] == wanted
    member = jnp.sum(hit.astype(jnp.int32), axis=2)
    slot = jnp.cumsum(member, axis=1) - member
    gate = jnp.sum(jnp.where(hit, all_gates[:, :, :, None], 0.0), axis=2)
    return jnp.where(member > 0, slot, -1), gate


def expert_ffn(rows, w_one, w_three, w_two):
    first = jnp.einsum('end,edf->enf', rows, w_one, preferred_element_type=jnp.float32)
    third = jnp.einsum('end,edf->enf', rows, w_three, preferred_element_type=jnp.float32)
    activated = (jax.nn.silu(first) * third).astype(jnp.bfloat16)
    return jnp.einsum('enf,efd->end', activated, w_two, preferred_element_type=jnp.float32).astype(jnp.bfloat16)


def solution(mesh):
    tok_spec = P(('dp', 'ep'))
    row_spec = P('ep')

    def local_layer(tokens, w_query, w_key, w_value, w_out, w_router, w_one, w_three, w_two, expert_ids):
        seq_count, seq_len, model_dim = tokens.shape
        choices = expert_ids.shape[2]
        experts = w_router.shape[1]
        local_experts = w_one.shape[0]
        tok_count = seq_count * seq_len
        cap_rows = 2 * tok_count * choices // experts
        ids = expert_ids.reshape(tok_count, choices)
        all_ids = lax.all_gather(ids, 'ep', axis=0)
        full_query = lax.all_gather(w_query, 'ep', axis=0, tiled=True)
        full_key = lax.all_gather(w_key, 'ep', axis=0, tiled=True)
        full_value = lax.all_gather(w_value, 'ep', axis=0, tiled=True)
        full_out = lax.all_gather(w_out, 'ep', axis=0, tiled=True)
        hidden = attention_layer(tokens, full_query, full_key, full_value, full_out).reshape(tok_count, model_dim)
        normed, gates = router_gates(hidden, w_router, ids)
        all_normed = lax.all_gather(normed, 'ep', axis=0)
        all_gates = lax.all_gather(gates, 'ep', axis=0)
        first = lax.axis_index('ep') * local_experts
        slot, gate = local_tables(all_ids, all_gates, first, local_experts)
        place = slot[:, :, :, None] == jnp.arange(cap_rows, dtype=jnp.int32)
        rows = jnp.einsum('stec,std->secd', place.astype(jnp.bfloat16), all_normed, preferred_element_type=jnp.float32).astype(jnp.bfloat16)
        packed = rows.transpose(1, 0, 2, 3).reshape(local_experts, -1, model_dim)
        done = expert_ffn(packed, w_one, w_three, w_two)
        done = done.reshape(local_experts, -1, cap_rows, model_dim).transpose(1, 0, 2, 3)
        rest = jnp.where(place, gate[:, :, :, None], 0.0)
        mixed = 0.0
        for _ in range(3):
            part = lax.reduce_precision(rest, 8, 7)
            rest = rest - part
            mixed = mixed + jnp.einsum('stec,secd->std', part.astype(jnp.bfloat16), done, preferred_element_type=jnp.float32)
        total = lax.psum_scatter(mixed, 'ep', scatter_dimension=0, tiled=False)
        layer_out = (hidden.astype(jnp.float32) + total).astype(jnp.bfloat16)
        return layer_out.reshape(seq_count, seq_len, model_dim)

    return jax.shard_map(local_layer, mesh=mesh, in_specs=(tok_spec, row_spec, row_spec, row_spec, row_spec, P(), row_spec, row_spec, row_spec, tok_spec), out_specs=tok_spec, check_vma=False)
```

time: 1510 us -> 958 us (0.63)
  blocking collectives: 374 us -> 23.5 us
  local copies, waits for them, and re-layouts: 281 us -> 29.3 us
  matrix products: 227 us -> 339 us
  waiting for transfers between devices: 525 us -> 468 us
    all_to_all x1 -> x0, blocking collectives: 374 us -> none  [local_layer(): recv_rows = lax.all_to_all(send_rows, 'ep', 0, 1, tiled=True)]
    all_to_all x1 -> x0, waiting for transfers between devices: 293 us -> none  [local_layer(): back_rows = lax.all_to_all(done_rows, 'ep', 1, 0, tiled=True)]
    reduce_scatter x0 -> x1, waiting for transfers between devices: none -> 196 us  [local_layer(): total = lax.psum_scatter(mixed, 'ep', scatter_dimension=0, tiled=False)]
    gather x13 -> x0, local copies, waits for them, and re-layouts: 159 us -> none  [the longest x1 95.9 us: combine_rows(): picked = jnp.take(table, flat_slot, axis=0)]
    dot_general x2 -> x5, matrix products: 25.9 us -> 136 us  [the longest x3 105 us: local_layer(): jnp.einsum('stec,secd->std', part.astype(jnp.bfloat16), done, preferred_e...]
    all_to_all x2 -> x0, local copies, waits for them, and re-layouts: 52.9 us -> none  [the longest x1 30 us: local_layer(): back_rows = lax.all_to_all(done_rows, 'ep', 1, 0, tiled=True)]
    convert_element_type x2 -> x1, local copies, waits for them, and re-layouts: 60 us -> 22.9 us  [local_layer(): jnp.einsum('stec,std->secd', place.astype(jnp.bfloat16), all_normed, pref...]
    all_gather x0 -> x2, blocking collectives: none -> 23.5 us  [the longest x1 12 us: local_layer(): all_gates = lax.all_gather(gates, 'ep', axis=0)]
  transfers between devices with their start and end apart: 5 -> 6, of which waited for: 5 -> 6; matrix products, arithmetic and copies ran while one was open for 12% -> 14% of each run, Pallas kernels for 0% -> 0%
where the time goes in v1:
time: 958 us; the launch traced here: 948 us
  waiting for transfers between devices  468 us (49%)
  matrix products  339 us (35%)
  other arithmetic  73.1 us (8%)
  local copies, waits for them, and re-layouts  29.3 us (3%)
  blocking collectives  23.5 us (2%)
  between operations  14 us (1%)
    reduce_scatter x1, waiting for transfers between devices, local_layer(): total = lax.psum_scatter(mixed, 'ep', scatter_dimension=0, tiled=False)  196 us
    dot_general x3, matrix products, local_layer(): jnp.einsum('stec,secd->std', part.astype(jnp.bfloat16), done, preferred_e...  105 us
    all_gather x1, waiting for transfers between devices, local_layer(): full_query = lax.all_gather(w_query, 'ep', axis=0, tiled=True)  84.5 us
    all_gather x1, waiting for transfers between devices, local_layer(): full_key = lax.all_gather(w_key, 'ep', axis=0, tiled=True)  71.4 us
    all_gather x1, waiting for transfers between devices, local_layer(): full_out = lax.all_gather(w_out, 'ep', axis=0, tiled=True)  64.1 us
    dot_general x1, matrix products, expert_ffn(): jnp.einsum('end,edf->enf', rows, w_three, preferred_element_type=jnp.floa...  49.4 us
    dot_general x1, matrix products, expert_ffn(): jnp.einsum('end,edf->enf', rows, w_one, preferred_element_type=jnp.float32)  41 us
    dot_general x1, matrix products, expert_ffn(): jnp.einsum('enf,efd->end', activated, w_two, preferred_element_type=jnp.f...  39.1 us
  transfers between devices with their start and end apart: 6, of which 6 were waited for; matrix products, arithmetic and copies ran while one was open for 14% of the time, Pallas kernels for 0%

profile of v1, /device:TPU:0, one launch (start us, length us, event | category | flops | bytes accessed | tf_op | source)
XLA Modules:
  0.0 947.5 jit_solution(3335107315697963689)
XLA Ops:
  9.5 2.1 fusion.45
  11.6 84.5 %all-gather.8.cloned.1.call-done = bf16[2048,32,128]{2,1,0:T(8,128)(2,1)} async-done(((bf16[256,32,128]{2,1,0:T(8,128)(2,1)}), bf16[2048,32,128]{2,1,0:T(8,128)(2,1)}) %all-gather.8.cloned.1.call-update) | async-done | bytes 16777232 | tf_op jit(solution)/shard_map/all_gather | solution.py:67
  96.1 14.5 %fusion.18 = bf16[512,32,128]{2,0,1:T(8,128)(2,1)} fusion(bf16[2048,32,128]{2,1,0:T(8,128)(2,1)} %all-gather.8.cloned.1.call-done, bf16[1,512,2048]{2,1,0:T(8,128)(2,1)} %param.10, f32[512]{0:T(512)S(1)} %add_rsqrt_fusion.1), kind=kOutput, calls=%fused_computation.28 | convolution fusion | flops 8593080320 | bytes 23070720 | tf_op jit(solution)/shard_map/bsd,dhk->bshk/dot_general | solution.py:19
  110.6 71.4 %all-gather.10.cloned.1.call-done = bf16[2048,32,128]{2,1,0:T(8,128)(2,1)} async-done(((bf16[256,32,128]{2,1,0:T(8,128)(2,1)}), bf16[2048,32,128]{2,1,0:T(8,128)(2,1)}) %all-gather.10.cloned.1.call-update) | async-done | bytes 16777232 | tf_op jit(solution)/shard_map/all_gather | solution.py:68
  182.0 22.9 %fusion.50 = f32[32,512,512]{1,2,0:T(8,128)} fusion(bf16[2048,32,128]{2,1,0:T(8,128)(2,1)} %all-gather.10.cloned.1.call-done, bf16[512,32,128]{2,0,1:T(8,128)(2,1)} %fusion.18, bf16[1,512,2048]{2,1,0:T(8,128)(2,1)S(1)} %copy-done.4, f32[512]{0:T(512)S(1)} %add_rsqrt_fusion.1), kind=kOutput, calls=%fused_computation.64 | convolution fusion | flops 10742661120 | bytes 56625152 | tf_op jit(solution)/shard_map/bqhk,bshk->bhqs/dot_general | solution.py:22
  204.9 34.1 %fusion.88 = (f32[32,512]{1,0:T(8,128)S(1)}, f32[32,512,512]{1,2,0:T(8,128)}) fusion(f32[32,512,512]{1,2,0:T(8,128)} %fusion.50, pred[512,512]{0,1:T(8,128)(4,1)S(1)} %iota_compare_fusion.3), kind=kOutput, calls=%fused_computation.98 | output fusion | flops 50332160 | bytes 67436544 | tf_op jit(solution)/shard_map/sub | solution.py:24
  239.0 28.9 %all-gather.6.cloned.1.call-done = bf16[2048,32,128]{2,1,0:T(8,128)(2,1)} async-done(((bf16[256,32,128]{2,1,0:T(8,128)(2,1)}), bf16[2048,32,128]{2,1,0:T(8,128)(2,1)}) %all-gather.6.cloned.1.call-update) | async-done | bytes 16777232 | tf_op jit(solution)/shard_map/all_gather | solution.py:69
  267.9 21.7 %fusion.62 = bf16[32,128,512]{2,1,0:T(8,128)(2,1)} fusion(f32[32,512,512]{1,2,0:T(8,128)} %get-tuple-element.6, f32[32,512]{1,0:T(8,128)S(1)} %get-tuple-element.5, bf16[2048,32,128]{2,1,0:T(8,128)(2,1)} %all-gather.6.cloned.1.call-done, bf16[1,512,2048]{2,1,0:T(8,128)(2,1)S(1)} %copy-done.4, f32[512]{0:T(512)S(1)} %add_rsqrt_fusion.1), kind=kOutput, calls=%fused_computation.68 | convolution fusion | flops 10761535488 | bytes 56690688 | tf_op jit(solution)/shard_map/bhqs,bshk->bqhk/dot_general | solution.py:25
  289.6 64.1 %all-gather.12.cloned.1.call-done = bf16[4096,2048]{1,0:T(8,128)(2,1)} async-done(((bf16[512,2048]{1,0:T(8,128)(2,1)}), bf16[4096,2048]{1,0:T(8,128)(2,1)}) %all-gather.12.cloned.1.call-update) | async-done | bytes 16777232 | tf_op jit(solution)/shard_map/all_gather | solution.py:70
  353.7 14.2 %fusion.42 = (f32[512]{0:T(512)S(1)}, bf16[1,512,2048]{2,1,0:T(8,128)(2,1)S(1)}) fusion(bf16[512,4096]{0,1:T(8,128)(2,1)} %bitcast.107, bf16[4096,2048]{1,0:T(8,128)(2,1)} %all-gather.12.cloned.1.call-done, bf16[1,512,2048]{2,1,0:T(8,128)(2,1)} %param.10), kind=kOutput, calls=%fused_computation.57 | convolution fusion | flops 8596226048 | bytes 25167872 | tf_op jit(solution)/shard_map/crd,de->cre/dot_general | solution.py:26
  367.9 2.0 fusion.48
  370.0 11.5 %all_gather.27 = s32[8,512,8]{1,2,0:T(8,128)S(1)} all-gather(s32[1,512,8]{1,2,0:T(8,128)S(1)} %copy-done.7), channel_id=1, replica_groups=mesh['dp'=1,'ep'=8] {'ep'}, dimensions={0}, use_global_device_ids=true | all-gather | bytes 147456 | tf_op jit(solution)/shard_map/all_gather | solution.py:66
  383.0 17.7 %reduce-window.6 = s32[8,16,4,128]{3,1,2,0:T(8,128)} reduce-window(s32[8,16,4,128]{3,1,2,0:T(8,128)} %copy_bitcast_fusion, s32[]{:T(128)} %constant.17.clone.1), window={size=1x1x1x128 pad=0_0x0_0x0_0x127_0}, to_apply=%region_4.5 | reduce-window | flops 8323072 | bytes 524292 | tf_op jit(solution)/shard_map/reduce-window
  400.6 1.8 slice.8
  402.4 1.8 copy.58
  405.6 0.8 copy.61
  406.4 1.8 fusion.72
  408.2 4.1 fusion.43
  412.3 8.2 select_reduce_fusion
  421.0 12.0 %all_gather.28 = f32[8,512,8]{1,2,0:T(8,128)S(1)} all-gather(f32[1,512,8]{1,2,0:T(8,128)S(1)} %fusion.74), channel_id=1, replica_groups=mesh['dp'=1,'ep'=8] {'ep'}, dimensions={0}, use_global_device_ids=true | all-gather | bytes 147456 | tf_op jit(solution)/shard_map/all_gather | solution.py:74
  433.1 1.6 fusion.68
  434.7 20.5 %all-gather.14.cloned.1.call-done = bf16[8,512,2048]{2,1,0:T(8,128)(2,1)} async-done(((bf16[1,512,2048]{2,1,0:T(8,128)(2,1)}), bf16[8,512,2048]{2,1,0:T(8,128)(2,1)}) %all-gather.14.cloned.1.call-update) | async-done | bytes 16777232 | tf_op jit(solution)/shard_map/all_gather | solution.py:73
  455.1 27.5 %convert_bitcast_fusion = bf16[16,8,64,2048]{3,2,0,1:T(8,128)(2,1)} fusion(bf16[8,512,2048]{2,1,0:T(8,128)(2,1)} %all-gather.14.cloned.1.call-done, s32[8,512,16]{1,2,0:T(8,128)} %fusion.72), kind=kOutput, calls=%fused_computation.9 | convolution fusion | flops 17200840704 | bytes 50593792 | tf_op jit(solution)/shard_map/stec,std->secd/dot_general | solution.py:78
  482.6 22.9 %copy.63 = bf16[16,8,64,2048]{3,2,1,0:T(8,128)(2,1)} copy(bf16[16,8,64,2048]{3,2,0,1:T(8,128)(2,1)} %convert_bitcast_fusion) | data formatting | bytes 67108864 | tf_op jit(solution)/shard_map/convert_element_type | solution.py:78
  505.6 41.0 %fusion.89 = f32[16,512,768]{2,1,0:T(8,128)} fusion(bf16[16,512,2048]{2,1,0:T(8,128)(2,1)} %bitcast.101, bf16[16,2048,768]{2,1,0:T(8,128)(2,1)} %param.16), kind=kOutput, calls=%fused_computation.99 | convolution fusion | flops 25769803776 | bytes 109051904 | tf_op jit(solution)/shard_map/end,edf->enf/dot_general | solution.py:48
  546.6 49.4 %multiply_convert_fusion.4 = bf16[16,512,768]{2,1,0:T(8,128)(2,1)} fusion(f32[16,512,768]{2,1,0:T(8,128)} %fusion.89, bf16[16,512,2048]{2,1,0:T(8,128)(2,1)} %bitcast.102, bf16[16,2048,768]{2,1,0:T(8,128)(2,1)} %param.17), kind=kOutput, calls=%fused_computation.17.clone.clone.1 | convolution fusion | flops 25807552512 | bytes 121634816 | tf_op jit(solution)/shard_map/end,edf->enf/dot_general | solution.py:49
  596.0 39.1 %convolution_convert_fusion = bf16[16,512,2048]{2,1,0:T(8,128)(2,1)} fusion(bf16[16,768,2048]{2,1,0:T(8,128)(2,1)} %param.18, bf16[16,512,768]{2,1,0:T(8,128)(2,1)} %multiply_convert_fusion.4), kind=kOutput, calls=%fused_computation.22 | convolution fusion | flops 25786580992 | bytes 96468992 | tf_op jit(solution)/shard_map/enf,efd->end/dot_general | solution.py:51
  635.1 28.9 %fusion.1 = f32[8,512,2048,1]{2,1,3,0:T(8,128)} fusion(bf16[16,8,64,2048]{3,2,1,0:T(8,128)(2,1)} %bitcast.104, f32[8,512,16]{1,2,0:T(8,128)S(1)} %copy-done.6, s32[8,512,16]{1,2,0:T(8,128)S(1)} %copy-done.5), kind=kOutput, calls=%fused_computation.3 | convolution fusion | flops 17213423616 | bytes 67633152 | tf_op jit(solution)/shard_map/stec,secd->std/dot_general | solution.py:87
  664.0 29.1 %fusion.3 = f32[8,512,2048,1]{2,1,3,0:T(8,128)} fusion(bf16[16,8,64,2048]{3,2,1,0:T(8,128)(2,1)} %bitcast.105, f32[8,512,16]{1,2,0:T(8,128)S(1)} %copy-done.6, s32[8,512,16]{1,2,0:T(8,128)S(1)} %copy-done.5), kind=kOutput, calls=%fused_computation.5 | convolution fusion | flops 17205035008 | bytes 67633152 | tf_op jit(solution)/shard_map/stec,secd->std/dot_general | solution.py:87
  693.1 46.6 %bitcast_add_fusion = f32[8,512,2048]{2,1,0:T(8,128)} fusion(f32[8,512,2048,1]{2,1,3,0:T(8,128)} %fusion.1, f32[8,512,2048,1]{2,1,3,0:T(8,128)} %fusion.3, bf16[16,8,64,2048]{3,2,1,0:T(8,128)(2,1)} %bitcast.106, f32[8,512,16]{1,2,0:T(8,128)S(1)} %copy-done.6, s32[8,512,16]{1,2,0:T(8,128)S(1)} %copy-done.5), kind=kOutput, calls=%fused_computation.1 | convolution fusion | flops 17213423616 | bytes 134742016 | tf_op jit(solution)/shard_map/stec,secd->std/dot_general | solution.py:87
  739.7 196.4 %reduce-scatter.2.cloned.1.call-done = f32[1,512,2048]{2,1,0:T(8,128)} async-done(((f32[8,512,2048]{2,1,0:T(8,128)}), f32[1,512,2048]{2,1,0:T(8,128)}) %reduce-scatter.2.cloned.1.call-update) | async-done | bytes 4194320 | tf_op jit(solution)/shard_map/reduce_scatter | solution.py:88
  936.1 4.2 fusion.49
  (45 shorter events, 6.3 us)
Async XLA Ops:
  6.5 401.6 %copy-start = (f32[2048,128]{1,0:T(8,128)S(1)}, f32[2048,128]{1,0:T(8,128)}, u32[]{:S(2)}) copy-start(f32[2048,128]{1,0:T(8,128)} %param.15) | copy-start | bytes 3145732
  6.5 89.6 %all-gather.8.cloned.1.call-start = ((), (), s32[]{:S(2)}) async-start(), calls=%async_computation.2 | async-start | bytes 18874368 | tf_op jit(solution)/shard_map/all_gather | solution.py:67
  7.3 174.8 %all-gather.10.cloned.1.call-start = ((), (), s32[]{:S(2)}) async-start(), calls=%async_computation.3 | async-start | bytes 18874368 | tf_op jit(solution)/shard_map/all_gather | solution.py:68
  8.0 259.9 %all-gather.6.cloned.1.call-start = ((), (), s32[]{:S(2)}) async-start(), calls=%async_computation.1 | async-start | bytes 18874368 | tf_op jit(solution)/shard_map/all_gather | solution.py:69
  8.7 345.0 %all-gather.12.cloned.1.call-start = ((), (), s32[]{:S(2)}) async-start(), calls=%async_computation.4 | async-start | bytes 18874368 | tf_op jit(solution)/shard_map/all_gather | solution.py:70
  9.3 445.8 %all-gather.14.cloned.1.call-start = ((), (), s32[]{:S(2)}) async-start(), calls=%async_computation.5 | async-start | bytes 18874368 | tf_op jit(solution)/shard_map/all_gather | solution.py:73
  11.5 170.5 %copy-start.4 = (bf16[1,512,2048]{2,1,0:T(8,128)(2,1)S(1)}, bf16[1,512,2048]{2,1,0:T(8,128)(2,1)}, u32[]{:S(2)}) copy-start(bf16[1,512,2048]{2,1,0:T(8,128)(2,1)} %param.10) | copy-start | bytes 6291460
  353.7 16.3 %copy-start.7 = (s32[1,512,8]{1,2,0:T(8,128)S(1)}, s32[1,512,8]{1,2,0:T(8,128)}, u32[]{:S(2)}) copy-start(s32[1,512,8]{1,2,0:T(8,128)} %param.19) | copy-start | bytes 49156
  367.9 114.7 %copy-start.2 = (bf16[1,512,2048]{2,1,0:T(8,128)(2,1)}, bf16[1,512,2048]{2,1,0:T(8,128)(2,1)S(1)}, u32[]{:S(2)}) copy-start(bf16[1,512,2048]{2,1,0:T(8,128)(2,1)S(1)} %get-tuple-element.8) | copy-start | bytes 6291460
  367.9 13.5 %copy-start.8 = (f32[512]{0:T(512)}, f32[512]{0:T(512)S(1)}, u32[]{:S(2)}) copy-start(f32[512]{0:T(512)S(1)} %add_rsqrt_fusion) | copy-start | bytes 6148
  369.9 566.1 %reduce-scatter.2.cloned.1.call-start = ((), (), s32[]{:S(2)}) async-start(), calls=%async_computation.6 | async-start | bytes 37748736 | tf_op jit(solution)/shard_map/reduce_scatter | solution.py:88
  381.5 0.5 copy-start.9
  596.0 39.1 %copy-start.5 = (s32[8,512,16]{1,2,0:T(8,128)S(1)}, s32[8,512,16]{1,2,0:T(8,128)}, u32[]{:S(2)}) copy-start(s32[8,512,16]{1,2,0:T(8,128)} %fusion.72) | copy-start | bytes 786436
  596.0 39.1 %copy-start.6 = (f32[8,512,16]{1,2,0:T(8,128)S(1)}, f32[8,512,16]{1,2,0:T(8,128)}, u32[]{:S(2)}) copy-start(f32[8,512,16]{1,2,0:T(8,128)} %fusion.68) | copy-start | bytes 786436
  739.7 200.6 %copy-start.1 = (f32[2048,128]{1,0:T(8,128)S(1)}, f32[2048,128]{1,0:T(8,128)}, u32[]{:S(2)}) copy-start(f32[2048,128]{1,0:T(8,128)} %param.15) | copy-start | bytes 3145732
  739.7 196.4 %copy-start.3 = (bf16[1,512,2048]{2,1,0:T(8,128)(2,1)S(1)}, bf16[1,512,2048]{2,1,0:T(8,128)(2,1)}, u32[]{:S(2)}) copy-start(bf16[1,512,2048]{2,1,0:T(8,128)(2,1)} %copy-done.2) | copy-start | bytes 6291460
Sparse Core Ops, SparseCore 0:
  9.2 86.8 all-gather.7
  97.9 84.0 all-gather.9
  183.8 84.0 all-gather.5
  269.6 84.0 all-gather.11
  370.1 85.0 all-gather.13
  739.8 196.1 reduce-scatter.1

commit v2 on v0

v2 whole, which is shorter than its diff:
```python
import functools

import jax
import jax.numpy as jnp
from jax import lax
from jax.experimental import pallas as pl
from jax.experimental.pallas import tpu as pltpu
from jax.sharding import PartitionSpec as P

EPS = 1e-6
CAP = 64
UNIT = 16
VMEM_MAX = 67043328


def rms_norm(vals):
    wide = vals.astype(jnp.float32)
    return wide * lax.rsqrt(jnp.mean(wide * wide, axis=-1, keepdims=True) + EPS)


def attention_layer(tokens, w_query, w_key, w_value, w_out):
    seq_count = tokens.shape[0]
    seq_len = tokens.shape[1]
    head_dim = w_query.shape[2]
    normed = rms_norm(tokens).astype(jnp.bfloat16)
    query = jnp.einsum('bsd,dhk->bshk', normed, w_query, preferred_element_type=jnp.float32).astype(jnp.bfloat16)
    keys = jnp.einsum('bsd,dhk->bshk', normed, w_key, preferred_element_type=jnp.float32).astype(jnp.bfloat16)
    values = jnp.einsum('bsd,dhk->bshk', normed, w_value, preferred_element_type=jnp.float32).astype(jnp.bfloat16)
    scores = jnp.einsum('bqhk,bshk->bhqs', query, keys, preferred_element_type=jnp.float32) * head_dim ** -0.5
    causal = lax.broadcasted_iota(jnp.int32, (seq_len, seq_len), 0) >= lax.broadcasted_iota(jnp.int32, (seq_len, seq_len), 1)
    attn_weights = jax.nn.softmax(jnp.where(causal, scores, -jnp.inf), axis=-1).astype(jnp.bfloat16)
    context = jnp.einsum('bhqs,bshk->bqhk', attn_weights, values, preferred_element_type=jnp.float32).astype(jnp.bfloat16)
    attn_out = jnp.einsum('crd,de->cre', context.reshape(seq_count, seq_len, -1), w_out, preferred_element_type=jnp.float32)
    return (tokens.astype(jnp.float32) + attn_out).astype(jnp.bfloat16)


def router_gates(hidden, w_router, ids_t):
    normed = rms_norm(hidden)
    logits = jnp.einsum('td,de->et', normed, w_router, precision=lax.Precision.HIGHEST, preferred_element_type=jnp.float32)
    hit = ids_t[:, None, :] == jnp.arange(w_router.shape[1], dtype=jnp.int32)[None, :, None]
    chosen = jnp.sum(jnp.where(hit, logits[None], 0.0), axis=1)
    return normed.astype(jnp.bfloat16), jax.nn.softmax(chosen, axis=0)


def neighbours():
    me = lax.axis_index('ep')
    core, chip = lax.rem(me, 2), me // 2
    side, up = lax.rem(chip, 2), chip // 2
    return me, core, chip, 1 - side + 2 * up, side + 2 * (1 - up), 3 - chip


def greet(devices):
    barrier = pltpu.get_barrier_semaphore()
    for device in devices:
        pl.semaphore_signal(barrier, inc=1, device_id={'ep': device}, device_id_type=pl.DeviceIdType.MESH)
    pl.semaphore_wait(barrier, len(devices))


def remote(src, dst, send_sem, recv_sem, device):
    return pltpu.make_async_remote_copy(src_ref=src, dst_ref=dst, send_sem=send_sem, recv_sem=recv_sem, device_id={'ep': device}, device_id_type=pl.DeviceIdType.MESH)


def spread_kernel(u_hbm, g_hbm, slot_ref, x_hbm, gall_hbm, ubuf, hbuf, xbuf, own_sem, gown_sem, out_sem, x_send, y_send, d_send, recv, g_send, g_recv):
    me, core, chip, xn, yn, dg = neighbours()
    mate = me + 1 - 2 * core
    tok = ubuf.shape[1]
    part = tok // 4
    local_experts = slot_ref.shape[1]
    x_dev, y_dev, dg_dev = xn * 2 + core, yn * 2 + core, dg * 2 + core
    others = (x_dev, y_dev, mate, dg_dev, xn * 2 + 1 - core, yn * 2 + 1 - core, dg * 2 + 1 - core)
    greet(others)

    def rows(piece):
        return pl.ds(piece * part, part)

    def landed(source, piece):
        remote(ubuf.at[source, rows(piece)], ubuf.at[source, rows(piece)], d_send.at[0, 0], recv.at[source, piece], mate).wait_recv()

    def pass_on(order, source, piece):
        return remote(ubuf.at[source, rows(piece)], ubuf.at[source, rows(piece)], d_send.at[order, piece], recv.at[source, piece], mate)

    def across_x(slot, source, piece, src):
        return remote(src, ubuf.at[source, rows(piece)], x_send.at[slot], recv.at[source, piece], x_dev)

    def across_y(slot, source, piece, src):
        return remote(src, ubuf.at[source, rows(piece)], y_send.at[slot], recv.at[source, piece], y_dev)

    own = pltpu.make_async_copy(u_hbm, ubuf.at[me], own_sem)
    own.start()
    gown = pltpu.make_async_copy(g_hbm, gall_hbm.at[me], gown_sem)
    gown.start()
    for slot in range(4):
        across_x(slot, me, slot, u_hbm.at[rows(slot)]).start()
        across_y(slot, me, (slot + 2) % 4, u_hbm.at[rows((slot + 2) % 4)]).start()
    for piece in range(4):
        remote(u_hbm.at[rows(piece)], ubuf.at[me, rows(piece)], d_send.at[0, piece], recv.at[me, piece], mate).start()
    for slot, device in enumerate(others):
        remote(g_hbm, gall_hbm.at[me], g_send.at[slot], g_recv.at[me], device).start()
    own.wait()

    def out_copy(order, source):
        return pltpu.make_async_copy(xbuf.at[lax.rem(order, 2)], x_hbm.at[:, source], out_sem.at[lax.rem(order, 2)])

    def step(order, carry):
        kind = order // 2
        base = jnp.where(kind == 0, chip, jnp.where(kind == 1, xn, jnp.where(kind == 2, yn, dg)))
        odd = lax.rem(order, 2)
        source = base * 2 + core + odd * (1 - 2 * core)

        @pl.when(order == 2)
        def _():
            for piece in (0, 1):
                landed(x_dev, piece)
                across_y(4 + piece, x_dev, piece, ubuf.at[x_dev, rows(piece)]).start()
                pass_on(1, x_dev, piece).start()
                landed(y_dev, piece + 2)
                across_x(4 + piece, y_dev, piece + 2, ubuf.at[y_dev, rows(piece + 2)]).start()
                pass_on(2, y_dev, piece + 2).start()
            for piece in (0, 1):
                landed(x_dev, piece + 2)
                pass_on(1, x_dev, piece + 2).start()
                landed(y_dev, piece)
                pass_on(2, y_dev, piece).start()

        @pl.when(order == 6)
        def _():
            for piece in (0, 2, 1, 3):
                landed(dg_dev, piece)
                pass_on(3, dg_dev, piece).start()

        @pl.when(odd == 1)
        def _():
            for piece in range(4):
                landed(source, piece)

        @pl.when(order >= 2)
        def _():
            out_copy(order, source).wait()

        spot = lax.broadcasted_iota(jnp.int32, (CAP, tok), 0)
        for expert in range(local_experts):
            hit = slot_ref[source, expert:expert + 1, :] == spot
            hbuf[expert * CAP:(expert + 1) * CAP, :] = jnp.where(hit, 1.0, 0.0).astype(jnp.bfloat16)
        width = 256

        def tile(n, c):
            cols = pl.ds(pl.multiple_of(n * width, width), width)
            picked = jnp.dot(hbuf[...], ubuf[source, :, cols], preferred_element_type=jnp.float32)
            xbuf[odd, :, :, cols] = picked.astype(jnp.bfloat16).reshape(local_experts, CAP, width)
            return c

        lax.fori_loop(0, ubuf.shape[2] // width, tile, 0)
        out_copy(order, source).start()
        return carry

    lax.fori_loop(0, 8, step, 0)
    out_copy(0, me).wait()
    out_copy(1, me).wait()
    gown.wait()
    for slot in range(4):
        across_x(slot, me, slot, u_hbm.at[rows(slot)]).wait_send()
        across_y(slot, me, slot, u_hbm.at[rows(slot)]).wait_send()
    for piece in (0, 1):
        across_y(4 + piece, x_dev, piece, ubuf.at[x_dev, rows(piece)]).wait_send()
        across_x(4 + piece, y_dev, piece + 2, ubuf.at[y_dev, rows(piece + 2)]).wait_send()
    for order, source in enumerate((me, x_dev, y_dev, dg_dev)):
        for piece in range(4):
            pass_on(order, source, piece).wait_send()
    for slot, device in enumerate(others):
        remote(g_hbm, gall_hbm.at[me], g_send.at[slot], g_recv.at[me], device).wait_send()
        remote(g_hbm, gall_hbm.at[device], g_send.at[slot], g_recv.at[device], device).wait_recv()


def spread(u, gates, slots):
    devices, local_experts, tok = slots.shape
    dim = u.shape[1]
    return pl.pallas_call(
        spread_kernel,
        out_shape=(jax.ShapeDtypeStruct((local_experts, devices, CAP, dim), jnp.bfloat16), jax.ShapeDtypeStruct((devices,) + gates.shape, jnp.float32)),
        in_specs=[pl.BlockSpec(memory_space=pl.ANY), pl.BlockSpec(memory_space=pl.ANY), pl.BlockSpec(memory_space=pltpu.VMEM)],
        out_specs=(pl.BlockSpec(memory_space=pl.ANY), pl.BlockSpec(memory_space=pl.ANY)),
        scratch_shapes=[
            pltpu.VMEM((devices, tok, dim), jnp.bfloat16),
            pltpu.VMEM((local_experts * CAP, tok), jnp.bfloat16),
            pltpu.VMEM((2, local_experts, CAP, dim), jnp.bfloat16),
            pltpu.SemaphoreType.DMA, pltpu.SemaphoreType.DMA, pltpu.SemaphoreType.DMA((2,)),
            pltpu.SemaphoreType.DMA((6,)), pltpu.SemaphoreType.DMA((6,)), pltpu.SemaphoreType.DMA((4, 4)),
            pltpu.SemaphoreType.DMA((devices, 4)), pltpu.SemaphoreType.DMA((7,)), pltpu.SemaphoreType.DMA((devices,)),
        ],
        compiler_params=pltpu.CompilerParams(collective_id=1, has_side_effects=True, vmem_limit_bytes=VMEM_MAX),
        name='spread_rows',
    )(u, gates, slots)


def ffn_kernel(units_ref, x_ref, w1_ref, w3_ref, w2_ref, o_ref, packed, middle, done):
    expert = pl.program_id(0)
    devices = x_ref.shape[1]
    tile = 128
    total = 0
    for source in range(devices):
        count = units_ref[expert * devices + source]

        def pack(i, c, source=source, total=total):
            packed[pl.ds(pl.multiple_of((total + i) * UNIT, UNIT), UNIT), :] = x_ref[0, source, pl.ds(pl.multiple_of(i * UNIT, UNIT), UNIT), :]
            return c

        lax.fori_loop(0, count, pack, 0)
        total = total + count

    def run(t, c):
        rows = pl.ds(pl.multiple_of(t * tile, tile), tile)
        for n in range(w1_ref.shape[2] // 256):
            cols = slice(n * 256, (n + 1) * 256)
            first = jnp.dot(packed[rows, :], w1_ref[0, :, cols], preferred_element_type=jnp.float32)
            third = jnp.dot(packed[rows, :], w3_ref[0, :, cols], preferred_element_type=jnp.float32)
            middle[:, cols] = (first * jax.nn.sigmoid(first) * third).astype(jnp.bfloat16)
        for n in range(w2_ref.shape[2] // 512):
            cols = slice(n * 512, (n + 1) * 512)
            done[rows, cols] = jnp.dot(middle[...], w2_ref[0, :, cols], preferred_element_type=jnp.float32).astype(jnp.bfloat16)
        return c

    lax.fori_loop(0, (total * UNIT + tile - 1) // tile, run, 0)
    total = 0
    for source in range(devices):
        count = units_ref[expert * devices + source]

        def unpack(i, c, source=source, total=total):
            o_ref[0, source, pl.ds(pl.multiple_of(i * UNIT, UNIT), UNIT), :] = done[pl.ds(pl.multiple_of((total + i) * UNIT, UNIT), UNIT), :]
            return c

        def clear(i, c, source=source):
            o_ref[0, source, pl.ds(pl.multiple_of(i * UNIT, UNIT), UNIT), :] = jnp.zeros((UNIT, o_ref.shape[3]), jnp.bfloat16)
            return c

        lax.fori_loop(0, count, unpack, 0)
        lax.fori_loop(count, CAP // UNIT, clear, 0)
        total = total + count


def expert_ffn(units, x, w_one, w_three, w_two):
    experts, devices, _, dim = x.shape
    mid = w_one.shape[2]
    block = lambda *shape: pl.BlockSpec((1,) + shape, lambda e, units: (e,) + (0,) * len(shape))
    return pl.pallas_call(
        ffn_kernel,
        out_shape=jax.ShapeDtypeStruct(x.shape, jnp.bfloat16),
        grid_spec=pltpu.PrefetchScalarGridSpec(
            num_scalar_prefetch=1,
            grid=(experts,),
            in_specs=[block(devices, CAP, dim), block(dim, mid), block(dim, mid), block(mid, dim)],
            out_specs=block(devices, CAP, dim),
            scratch_shapes=[pltpu.VMEM((devices * CAP, dim), jnp.bfloat16), pltpu.VMEM((128, mid), jnp.bfloat16), pltpu.VMEM((devices * CAP, dim), jnp.bfloat16)],
        ),
        compiler_params=pltpu.CompilerParams(dimension_semantics=('arbitrary',), vmem_limit_bytes=VMEM_MAX),
        name='expert_mlp',
    )(units, x, w_one, w_three, w_two)


def combine_kernel(o_hbm, tab_hbm, h_hbm, y_ref, own, mate_rows, tab, gate3, p_one, r_one, p_two, r_two, p_last, r_last, own_sem, tab_sem, h_sem, mate_send, mate_recv, one_send, one_recv, two_send, two_recv, last_send, last_recv):
    me, core, chip, xn, yn, dg = neighbours()
    mate = me + 1 - 2 * core
    near = xn + core * (yn - xn)
    far = yn + core * (xn - yn)
    near_dev, far_dev = near * 2 + core, far * 2 + core
    half = own.shape[3]
    rows_n = p_one.shape[1]
    experts = own.shape[1]
    greet((near_dev, far_dev, mate))
    my_cols = pl.ds(pl.multiple_of(core * half, half), half)
    mate_cols = pl.ds(pl.multiple_of((1 - core) * half, half), half)

    def dest(i, first, second):
        pair = i // 2
        base = jnp.where(pair == 0, dg, jnp.where(pair == 1, first, jnp.where(pair == 2, second, chip)))
        return base

    def my_dest(i):
        odd = lax.rem(i, 2)
        return dest(i, near, far) * 2 + jnp.where(i < 6, odd, 1 - core + odd * (2 * core - 1))

    def mate_dest(i):
        odd = lax.rem(i, 2)
        return dest(i, far, near) * 2 + jnp.where(i < 6, odd, core + odd * (1 - 2 * core))

    def to_mate(i):
        return remote(o_hbm.at[:, mate_dest(i), :, mate_cols], mate_rows.at[i], mate_send.at[i], mate_recv.at[i], mate)

    def own_copy(i):
        return pltpu.make_async_copy(o_hbm.at[:, my_dest(i), :, my_cols], own.at[lax.rem(i, 2)], own_sem.at[lax.rem(i, 2)])

    def tab_copy(i):
        return pltpu.make_async_copy(tab_hbm.at[my_dest(i)], tab.at[lax.rem(i, 2)], tab_sem.at[lax.rem(i, 2)])

    def one_copy(n):
        return remote(p_one.at[n], r_one.at[n], one_send.at[n], one_recv.at[n], near_dev)

    def two_copy(n):
        return remote(p_two.at[n], r_two.at[n], two_send.at[n], two_recv.at[n], far_dev)

    def last_copy(n):
        return remote(p_last.at[n], r_last.at[n], last_send.at[n], last_recv.at[n], mate)

    own_copy(0).start()
    tab_copy(0).start()
    for i in range(8):
        to_mate(i).start()
    residual = pltpu.make_async_copy(h_hbm, y_ref, h_sem)
    residual.start()

    def open_dest(i):
        own_copy(i).wait()
        tab_copy(i).wait()
        to_mate(i).wait_recv()

        @pl.when(i < 7)
        def _():
            own_copy(i + 1).start()
            tab_copy(i + 1).start()

    def weights(i, part):
        slot = lax.rem(i, 2)
        cols = pl.ds(pl.multiple_of(part * rows_n, rows_n), rows_n)
        spot = lax.broadcasted_iota(jnp.int32, (2 * CAP, rows_n), 0)
        low = spot < CAP
        place = (spot - jnp.where(low, 0, CAP)).astype(jnp.float32)
        for pair in range(experts):
            at = tab[slot, 2 * pair:2 * pair + 2, cols]
            gate = tab[slot, 2 * experts + 2 * pair:2 * experts + 2 * pair + 2, cols]
            hit = jnp.where(low, at[0:1], at[1:2]) == place
            value = jnp.where(hit, jnp.where(low, gate[0:1], gate[1:2]), 0.0).T
            top = value.astype(jnp.bfloat16)
            rest = value - top.astype(jnp.float32)
            mid = rest.astype(jnp.bfloat16)
            low_part = (rest - mid.astype(jnp.float32)).astype(jnp.bfloat16)
            where = slice(pair * 2 * CAP, (pair + 1) * 2 * CAP)
            gate3[0:rows_n, where] = top
            gate3[rows_n:2 * rows_n, where] = mid
            gate3[2 * rows_n:3 * rows_n, where] = low_part

    def products(i, part, sink):
        weights(i, part)
        slot = lax.rem(i, 2)
        depth = experts * CAP
        width = 256

        def tile(n, c):
            cols = pl.ds(pl.multiple_of(n * width, width), width)
            mine = own[slot, :, :, cols].reshape(depth, width)
            other = mate_rows[i, :, :, cols].reshape(depth, width)
            out = jnp.dot(gate3[:, :depth], mine, preferred_element_type=jnp.float32) + jnp.dot(gate3[:, depth:], other, preferred_element_type=jnp.float32)
            sink(cols, out[0:rows_n] + out[rows_n:2 * rows_n] + out[2 * rows_n:3 * rows_n])
            return c

        lax.fori_loop(0, half // width, tile, 0)

    def phase_one(step, c):
        i, part = step // 2, lax.rem(step, 2)

        @pl.when(part == 0)
        def _():
            open_dest(i)

        def sink(cols, value):
            p_one[step, :, cols] = value

        products(i, part, sink)
        one_copy(step).start()
        return c

    lax.fori_loop(0, 8, phase_one, 0)

    def phase_two(step, c):
        i, part = 4 + step // 2, lax.rem(step, 2)

        @pl.when(part == 0)
        def _():
            open_dest(i)

        def sink(cols, value):
            p_two[step, :, cols] = value

        products(i, part, sink)
        one_copy(step).wait_recv()
        p_two[step] = p_two[step] + r_one[step]
        two_copy(step).start()
        return c

    lax.fori_loop(0, 4, phase_two, 0)
    residual.wait()

    def phase_three(step, c):
        i, part = 6 + step // 2, lax.rem(step, 2)

        @pl.when(part == 0)
        def _():
            open_dest(i)

        def sink(cols, value):
            p_last[step, :, cols] = value

        products(i, part, sink)
        target = jnp.where(step < 2, 1 - core, core)
        n = target * 2 + part
        one_copy(4 + n).wait_recv()
        two_copy(n).wait_recv()
        p_last[step] = p_last[step] + (r_one[4 + n] + r_two[n])

        @pl.when(step < 2)
        def _():
            last_copy(step).start()

        @pl.when(step >= 2)
        def _():
            rows = pl.ds(pl.multiple_of(part * rows_n, rows_n), rows_n)
            y_ref[rows, my_cols] = (y_ref[rows, my_cols].astype(jnp.float32) + p_last[step]).astype(jnp.bfloat16)

        return c

    lax.fori_loop(0, 4, phase_three, 0)
    for n in range(2):
        rows = pl.ds(n * rows_n, rows_n)
        last_copy(n).wait_recv()
        y_ref[rows, mate_cols] = (y_ref[rows, mate_cols].astype(jnp.float32) + r_last[n]).astype(jnp.bfloat16)
    for n in range(8):
        to_mate(n).wait_send()
        one_copy(n).wait_send()
    for n in range(4):
        two_copy(n).wait_send()
    for n in range(2):
        last_copy(n).wait_send()


def combine(done, tab, hidden):
    experts, devices, _, dim = done.shape
    tok = hidden.shape[0]
    half, part = dim // 2, tok // 2
    dma = pltpu.SemaphoreType.DMA
    return pl.pallas_call(
        combine_kernel,
        out_shape=jax.ShapeDtypeStruct((tok, dim), jnp.bfloat16),
        in_specs=[pl.BlockSpec(memory_space=pl.ANY)] * 3,
        out_specs=pl.BlockSpec(memory_space=pltpu.VMEM),
        scratch_shapes=[
            pltpu.VMEM((2, experts, CAP, half), jnp.bfloat16),
            pltpu.VMEM((devices, experts, CAP, half), jnp.bfloat16),
            pltpu.VMEM((2,) + tab.shape[1:], jnp.float32),
            pltpu.VMEM((3 * part, 2 * experts * CAP), jnp.bfloat16),
            pltpu.VMEM((8, part, half), jnp.float32),
            pltpu.VMEM((8, part, half), jnp.float32),
            pltpu.VMEM((4, part, half), jnp.float32),
            pltpu.VMEM((4, part, half), jnp.float32),
            pltpu.VMEM((4, part, half), jnp.float32),
            pltpu.VMEM((2, part, half), jnp.float32),
            dma((2,)), dma((2,)), dma, dma((8,)), dma((8,)), dma((8,)), dma((8,)), dma((4,)), dma((4,)), dma((2,)), dma((2,)),
        ],
        compiler_params=pltpu.CompilerParams(collective_id=2, has_side_effects=True, vmem_limit_bytes=VMEM_MAX),
        name='combine_rows',
    )(done, tab, hidden)


def solution(mesh):
    tok_spec = P(('dp', 'ep'))
    row_spec = P('ep')

    def local_layer(tokens, w_query, w_key, w_value, w_out, w_router, w_one, w_three, w_two, expert_ids):
        seq_count, seq_len, model_dim = tokens.shape
        choices = expert_ids.shape[2]
        local_experts = w_one.shape[0]
        tok_count = seq_count * seq_len
        ids_t = expert_ids.reshape(tok_count, choices).T
        all_ids = lax.all_gather(ids_t, 'ep', axis=0)
        me = lax.axis_index('ep')
        core = lax.rem(me, 2)
        local = jnp.arange(local_experts, dtype=jnp.int32)
        wanted = jnp.concatenate([me * local_experts + local, (me + 1 - 2 * core) * local_experts + local])
        hit = all_ids[:, :, None, :] == wanted[None, None, :, None]
        member = jnp.sum(hit.astype(jnp.int32), axis=1)
        before = jnp.arange(tok_count)[:, None] < jnp.arange(tok_count)[None, :]
        slot = jnp.einsum('set,tu->seu', member.astype(jnp.bfloat16), before.astype(jnp.bfloat16), preferred_element_type=jnp.float32)
        slot = jnp.where(member > 0, slot, -1.0)
        slots = slot[:, :local_experts].astype(jnp.int32)
        units = ((jnp.sum(member[:, :local_experts], axis=2) + UNIT - 1) // UNIT).T.reshape(-1)

        full_query = lax.all_gather(w_query, 'ep', axis=0, tiled=True)
        full_key = lax.all_gather(w_key, 'ep', axis=0, tiled=True)
        full_value = lax.all_gather(w_value, 'ep', axis=0, tiled=True)
        full_out = lax.all_gather(w_out, 'ep', axis=0, tiled=True)
        hidden = attention_layer(tokens, full_query, full_key, full_value, full_out).reshape(tok_count, model_dim)
        normed, gates = router_gates(hidden, w_router, ids_t)
        x, all_gates = spread(normed, gates, slots)
        gate = jnp.sum(jnp.where(hit, all_gates[:, :, None, :], 0.0), axis=1)
        tab = jnp.concatenate([slot, gate], axis=1)
        done = expert_ffn(units, x, w_one, w_three, w_two)
        layer_out = combine(done, tab, hidden)
        return layer_out.reshape(seq_count, seq_len, model_dim)

    return jax.shard_map(local_layer, mesh=mesh, in_specs=(tok_spec, row_spec, row_spec, row_spec, row_spec, P(), row_spec, row_spec, row_spec, tok_spec), out_specs=tok_spec, check_vma=False)
```

time: 1510 us -> 723 us (0.48)
  blocking collectives: 374 us -> 14.3 us
  Pallas kernels: 0 us -> 331 us
  waiting for transfers between devices: 525 us -> 234 us
  local copies, waits for them, and re-layouts: 281 us -> 4.76 us
  matrix products: 227 us -> 76.5 us
  other arithmetic: 72.8 us -> 44.4 us
    all_to_all x1 -> x0, blocking collectives: 374 us -> none  [local_layer(): recv_rows = lax.all_to_all(send_rows, 'ep', 0, 1, tiled=True)]
    pallas_call x0 -> x3, Pallas kernels: none -> 331 us  [the longest x1 158 us: combine(): pl.pallas_call(combine_kernel, out_shape=jax.ShapeDtypeStruct((tok, dim),...]
    all_to_all x1 -> x0, waiting for transfers between devices: 293 us -> none  [local_layer(): back_rows = lax.all_to_all(done_rows, 'ep', 1, 0, tiled=True)]
    gather x13 -> x0, local copies, waits for them, and re-layouts: 159 us -> none  [the longest x1 95.9 us: combine_rows(): picked = jnp.take(table, flat_slot, axis=0)]
    dot_general x5 -> x2, matrix products: 155 us -> 4.61 us  [the longest x1 3.49 us: router_gates(): jnp.einsum('td,de->et', normed, w_router, precision=lax.Precision.HIGHEST...]
    convert_element_type x2 -> x0, local copies, waits for them, and re-layouts: 60 us -> none  [the longest x1 30 us: expert_ffn(): jnp.einsum('enf,efd->end', activated, w_two, preferred_element_type=jnp.f...]
    all_to_all x2 -> x0, local copies, waits for them, and re-layouts: 52.9 us -> none  [the longest x1 30 us: local_layer(): back_rows = lax.all_to_all(done_rows, 'ep', 1, 0, tiled=True)]
    reduce_sum x3 -> x5, other arithmetic: 21.4 us -> 3.51 us  [the longest x1 1.59 us: local_layer(): gate = jnp.sum(jnp.where(hit, all_gates[:, :, None, :], 0.0), axis=1)]
  transfers between devices with their start and end apart: 5 -> 4, of which waited for: 5 -> 4; matrix products, arithmetic and copies ran while one was open for 12% -> 14% of each run, Pallas kernels for 0% -> 0%
where the time goes in v2:
time: 723 us; the launch traced here: 719 us
  Pallas kernels  331 us (46%)
  waiting for transfers between devices  234 us (32%)
  matrix products  76.5 us (11%)
  other arithmetic  44.4 us (6%)
  blocking collectives  14.3 us (2%)
  between operations  13.3 us (2%)
    pallas_call x1, Pallas kernels, combine(): pl.pallas_call(combine_kernel, out_shape=jax.ShapeDtypeStruct((tok, dim),...  158 us
    pallas_call x1, Pallas kernels, expert_ffn(): pl.pallas_call(ffn_kernel, out_shape=jax.ShapeDtypeStruct(x.shape, jnp.bf...  89.4 us
    pallas_call x1, Pallas kernels, spread(): pl.pallas_call(spread_kernel, out_shape=(jax.ShapeDtypeStruct((local_expe...  83.9 us
    all_gather x1, waiting for transfers between devices, local_layer(): full_key = lax.all_gather(w_key, 'ep', axis=0, tiled=True)  72 us
    all_gather x1, waiting for transfers between devices, local_layer(): full_query = lax.all_gather(w_query, 'ep', axis=0, tiled=True)  66.2 us
    all_gather x1, waiting for transfers between devices, local_layer(): full_out = lax.all_gather(w_out, 'ep', axis=0, tiled=True)  64.6 us
    sub x1, other arithmetic, attention_layer(): jax.nn.softmax(jnp.where(causal, scores, -jnp.inf), axis=-1)  34.1 us
    all_gather x1, waiting for transfers between devices, local_layer(): full_value = lax.all_gather(w_value, 'ep', axis=0, tiled=True)  28.9 us
  transfers between devices with their start and end apart: 4, of which 4 were waited for; matrix products, arithmetic and copies ran while one was open for 14% of the time, Pallas kernels for 0%

profile of v2, /device:TPU:0, one launch (start us, length us, event | category | flops | bytes accessed | tf_op | source)
XLA Modules:
  0.0 718.8 jit_solution(1038483138938400482)
XLA Ops:
  6.5 0.7 all-gather.8.cloned.1.call-update
  7.3 0.7 all-gather.10.cloned.1.call-update
  8.1 0.7 all-gather.6.cloned.1.call-update
  8.8 0.5 all-gather.12.cloned.1.call-update
  9.3 14.3 %all-gather = s32[64,512]{1,0:T(8,128)} all-gather(s32[8,512]{1,0:T(8,128)S(1)} %bitcast.50), channel_id=2, replica_groups=mesh['dp'=1,'ep'=8] {'ep'}, dimensions={0}, use_global_device_ids=true | all-gather | bytes 147456 | tf_op jit(solution)/shard_map/all_gather | solution.py:471
  23.8 0.5 copy-done.4
  24.3 1.4 fusion.15
  25.8 0.2 slice_reduce_fusion
  26.1 0.6 reshape.85.units_ref
  26.8 0.5 fusion.17
  27.3 1.1 convolution_select_fusion
  28.4 1.7 slice_convert_fusion.slot_ref
  30.0 66.2 %all-gather.8.cloned.1.call-done = bf16[2048,32,128]{2,1,0:T(8,128)(2,1)} async-done(((bf16[256,32,128]{2,1,0:T(8,128)(2,1)}), bf16[2048,32,128]{2,1,0:T(8,128)(2,1)}) %all-gather.8.cloned.1.call-update) | async-done | bytes 16777232 | tf_op jit(solution)/shard_map/all_gather | solution.py:484
  96.3 13.9 %fusion.4 = bf16[512,32,128]{2,0,1:T(8,128)(2,1)} fusion(bf16[2048,32,128]{2,1,0:T(8,128)(2,1)} %all-gather.8.cloned.1.call-done, bf16[1,512,2048]{2,1,0:T(8,128)(2,1)S(1)} %copy-done.1, f32[512]{0:T(512)S(1)} %add_rsqrt_fusion.1), kind=kOutput, calls=%fused_computation.7 | convolution fusion | flops 8593080320 | bytes 23070720 | tf_op jit(solution)/shard_map/bsd,dhk->bshk/dot_general | solution.py:26
  110.2 72.0 %all-gather.10.cloned.1.call-done = bf16[2048,32,128]{2,1,0:T(8,128)(2,1)} async-done(((bf16[256,32,128]{2,1,0:T(8,128)(2,1)}), bf16[2048,32,128]{2,1,0:T(8,128)(2,1)}) %all-gather.10.cloned.1.call-update) | async-done | bytes 16777232 | tf_op jit(solution)/shard_map/all_gather | solution.py:485
  182.2 22.9 %fusion.20 = f32[32,512,512]{1,2,0:T(8,128)} fusion(bf16[2048,32,128]{2,1,0:T(8,128)(2,1)} %all-gather.10.cloned.1.call-done, bf16[512,32,128]{2,0,1:T(8,128)(2,1)} %fusion.4, bf16[1,512,2048]{2,1,0:T(8,128)(2,1)S(1)} %copy-done.1, f32[512]{0:T(512)S(1)} %add_rsqrt_fusion.1), kind=kOutput, calls=%fused_computation.30 | convolution fusion | flops 10742661120 | bytes 56625152 | tf_op jit(solution)/shard_map/bqhk,bshk->bhqs/dot_general | solution.py:29
  205.1 34.1 %fusion.56 = (f32[32,512]{1,0:T(8,128)S(1)}, f32[32,512,512]{1,2,0:T(8,128)}) fusion(f32[32,512,512]{1,2,0:T(8,128)} %fusion.20, pred[512,512]{0,1:T(8,128)(4,1)S(1)} %iota_compare_fusion.2), kind=kOutput, calls=%fused_computation.68 | output fusion | flops 50332160 | bytes 67436544 | tf_op jit(solution)/shard_map/sub | solution.py:31
  239.2 28.9 %all-gather.6.cloned.1.call-done = bf16[2048,32,128]{2,1,0:T(8,128)(2,1)} async-done(((bf16[256,32,128]{2,1,0:T(8,128)(2,1)}), bf16[2048,32,128]{2,1,0:T(8,128)(2,1)}) %all-gather.6.cloned.1.call-update) | async-done | bytes 16777232 | tf_op jit(solution)/shard_map/all_gather | solution.py:486
  268.1 21.2 %fusion.33 = bf16[32,128,512]{2,1,0:T(8,128)(2,1)} fusion(f32[32,512,512]{1,2,0:T(8,128)} %get-tuple-element.10, f32[32,512]{1,0:T(8,128)S(1)} %get-tuple-element.9, bf16[2048,32,128]{2,1,0:T(8,128)(2,1)} %all-gather.6.cloned.1.call-done, bf16[1,512,2048]{2,1,0:T(8,128)(2,1)S(1)} %copy-done.1, f32[512]{0:T(512)S(1)} %add_rsqrt_fusion.1), kind=kOutput, calls=%fused_computation.35 | convolution fusion | flops 10761535488 | bytes 56690688 | tf_op jit(solution)/shard_map/bhqs,bshk->bqhk/dot_general | solution.py:32
  289.3 64.6 %all-gather.12.cloned.1.call-done = bf16[4096,2048]{1,0:T(8,128)(2,1)} async-done(((bf16[512,2048]{1,0:T(8,128)(2,1)}), bf16[4096,2048]{1,0:T(8,128)(2,1)}) %all-gather.12.cloned.1.call-update) | async-done | bytes 16777232 | tf_op jit(solution)/shard_map/all_gather | solution.py:487
  353.9 13.9 %fusion.14 = (f32[512]{0:T(512)S(1)}, bf16[512,2048]{1,0:T(8,128)(2,1)S(1)}) fusion(bf16[512,4096]{0,1:T(8,128)(2,1)} %bitcast.52, bf16[4096,2048]{1,0:T(8,128)(2,1)} %all-gather.12.cloned.1.call-done, bf16[1,512,2048]{2,1,0:T(8,128)(2,1)S(1)} %copy-done.1), kind=kOutput, calls=%fused_computation.24 | convolution fusion | flops 8596226048 | bytes 25167872 | tf_op jit(solution)/shard_map/crd,de->cre/dot_general | solution.py:33
  367.8 1.7 fusion.13.u_hbm
  369.5 0.3 copy-done
  369.8 3.5 fusion.40
  373.4 0.2 select_reduce_fusion
  373.7 0.6 fusion.44.g_hbm
  374.3 83.9 %spread_rows.1 = (bf16[16,8,64,2048]{3,2,1,0:T(8,128)(2,1)}, f32[8,8,512]{2,1,0:T(8,128)}) custom-call(bf16[512,2048]{1,0:T(8,128)(2,1)} %fusion.13.u_hbm, f32[8,512]{1,0:T(8,128)} %fusion.44.g_hbm, s32[8,16,512]{2,1,0:T(8,128)} %slice_convert_fusion.slot_ref), custom_call_target="tpu_custom_call" | custom-call | tf_op jit(solution)/shard_map/spread_rows/pallas_call | solution.py:177
  458.3 1.6 fusion.16
  459.9 2.1 pad_maximum_fusion.tab_hbm
  461.9 89.4 %expert_mlp.1.o_hbm = bf16[16,8,64,2048]{3,2,1,0:T(8,128)(2,1)} custom-call(s32[128]{0:T(128)} %reshape.85.units_ref, bf16[16,8,64,2048]{3,2,1,0:T(8,128)(2,1)} %get-tuple-element.7.x_ref, bf16[16,2048,768]{2,1,0:T(8,128)(2,1)} %w1_ref.1, bf16[16,2048,768]{2,1,0:T(8,128)(2,1)} %w3_ref.1, bf16[16,768,2048]{2,1,0:T(8,128)(2,1)} %w2_ref.1), custom_call_target="tpu_custom_call" | custom-call | tf_op jit(solution)/shard_map/expert_mlp/pallas_call | solution.py:244
  551.3 157.8 %combine_rows.1 = bf16[512,2048]{1,0:T(8,128)(2,1)} custom-call(bf16[16,8,64,2048]{3,2,1,0:T(8,128)(2,1)} %expert_mlp.1.o_hbm, f32[8,64,512]{2,1,0:T(8,128)} %pad_maximum_fusion.tab_hbm, bf16[512,2048]{1,0:T(8,128)(2,1)} %copy-done), custom_call_target="tpu_custom_call" | custom-call | tf_op jit(solution)/shard_map/combine_rows/pallas_call | solution.py:438
  709.1 3.2 copy.48
  (22 shorter events, 0.6 us)
Async XLA Ops:
  6.5 2.8 copy-start.3
  6.5 89.7 %all-gather.8.cloned.1.call-start = ((), (), s32[]{:S(2)}) async-start(), calls=%async_computation.1 | async-start | bytes 18874368 | tf_op jit(solution)/shard_map/all_gather | solution.py:484
  7.3 19.5 %copy-start.1 = (bf16[1,512,2048]{2,1,0:T(8,128)(2,1)S(1)}, bf16[1,512,2048]{2,1,0:T(8,128)(2,1)}, u32[]{:S(2)}) copy-start(bf16[1,512,2048]{2,1,0:T(8,128)(2,1)} %param.10) | copy-start | bytes 6291460
  7.3 174.9 %all-gather.10.cloned.1.call-start = ((), (), s32[]{:S(2)}) async-start(), calls=%async_computation.2 | async-start | bytes 18874368 | tf_op jit(solution)/shard_map/all_gather | solution.py:485
  8.0 260.1 %all-gather.6.cloned.1.call-start = ((), (), s32[]{:S(2)}) async-start(), calls=%async_computation | async-start | bytes 18874368 | tf_op jit(solution)/shard_map/all_gather | solution.py:486
  8.8 345.1 %all-gather.12.cloned.1.call-start = ((), (), s32[]{:S(2)}) async-start(), calls=%async_computation.3 | async-start | bytes 18874368 | tf_op jit(solution)/shard_map/all_gather | solution.py:487
  23.8 0.5 copy-start.4
  367.8 2.0 copy-start
  367.8 2.0 copy-start.2
Sparse Core Ops, SparseCore 0:
  9.2 87.0 all-gather.7
  98.1 84.0 all-gather.9
  184.0 84.0 all-gather.5
  269.8 84.0 all-gather.11

commit v3 on v2

--- a/solution.py
+++ b/solution.py
@@ -18,22 +18,6 @@
     return wide * lax.rsqrt(jnp.mean(wide * wide, axis=-1, keepdims=True) + EPS)
 
 
-def attention_layer(tokens, w_query, w_key, w_value, w_out):
-    seq_count = tokens.shape[0]
-    seq_len = tokens.shape[1]
-    head_dim = w_query.shape[2]
-    normed = rms_norm(tokens).astype(jnp.bfloat16)
-    query = jnp.einsum('bsd,dhk->bshk', normed, w_query, preferred_element_type=jnp.float32).astype(jnp.bfloat16)
-    keys = jnp.einsum('bsd,dhk->bshk', normed, w_key, preferred_element_type=jnp.float32).astype(jnp.bfloat16)
-    values = jnp.einsum('bsd,dhk->bshk', normed, w_value, preferred_element_type=jnp.float32).astype(jnp.bfloat16)
-    scores = jnp.einsum('bqhk,bshk->bhqs', query, keys, preferred_element_type=jnp.float32) * head_dim ** -0.5
-    causal = lax.broadcasted_iota(jnp.int32, (seq_len, seq_len), 0) >= lax.broadcasted_iota(jnp.int32, (seq_len, seq_len), 1)
-    attn_weights = jax.nn.softmax(jnp.where(causal, scores, -jnp.inf), axis=-1).astype(jnp.bfloat16)
-    context = jnp.einsum('bhqs,bshk->bqhk', attn_weights, values, preferred_element_type=jnp.float32).astype(jnp.bfloat16)
-    attn_out = jnp.einsum('crd,de->cre', context.reshape(seq_count, seq_len, -1), w_out, preferred_element_type=jnp.float32)
-    return (tokens.astype(jnp.float32) + attn_out).astype(jnp.bfloat16)
-
-
 def router_gates(hidden, w_router, ids_t):
     normed = rms_norm(hidden)
     logits = jnp.einsum('td,de->et', normed, w_router, precision=lax.Precision.HIGHEST, preferred_element_type=jnp.float32)
@@ -60,12 +44,280 @@
     return pltpu.make_async_remote_copy(src_ref=src, dst_ref=dst, send_sem=send_sem, recv_sem=recv_sem, device_id={'ep': device}, device_id_type=pl.DeviceIdType.MESH)
 
 
+def attend_kernel(tok_ref, ids_hbm, wq_hbm, wk_hbm, wv_hbm, wo_hbm, ctx_hbm, wfull_hbm, slots_ref, ids_ref, ids_buf, i_send, i_recv, i_own, nbuf, wbuf, wmate, qkv, cbuf, loc_sem, a_send, b_send, f_send, m_send, mf_send, w_recv, wm_recv, n_send, n_recv, c_send, c_recv, c_own, ox_send, oy_send, od_send, o_recv, o_own):
+    me, core, chip, xn, yn, dg = neighbours()
+    side = lax.rem(chip, 2)
+    mate = me + 1 - 2 * core
+    x_dev, y_dev, dg_dev, x_mate = xn * 2 + core, yn * 2 + core, dg * 2 + core, xn * 2 + 1 - core
+    weights = (wq_hbm, wk_hbm, wv_hbm)
+    seqs, tok, dim = nbuf.shape
+    group = wbuf.shape[3]
+    part = tok // 4
+    others = (x_dev, y_dev, mate, x_mate, dg_dev, yn * 2 + 1 - core, dg * 2 + 1 - core)
+    greet(others)
+
+    def cols(on_side, on_core):
+        return pl.ds(pl.multiple_of((2 * on_side + on_core) * group, group), group)
+
+    def local_w(m):
+        return pltpu.make_async_copy(weights[m].at[:, cols(side, core)], wbuf.at[m, me], loc_sem.at[m])
+
+    def own_mate(m):
+        return remote(weights[m].at[:, cols(side, 1 - core)], wbuf.at[m, me], m_send.at[m], w_recv.at[m, me], mate)
+
+    def over_x(m):
+        return (remote(weights[m].at[:, cols(1 - side, core)], wbuf.at[m, me], a_send.at[m, 0], w_recv.at[m, me], x_dev),
+                remote(weights[m].at[:, cols(1 - side, 1 - core)], wmate.at[m, 0], a_send.at[m, 1], wm_recv.at[m, 0], x_dev))
+
+    def over_y(m):
+        return (remote(weights[m].at[:, cols(side, core)], wbuf.at[m, me], b_send.at[m, 0], w_recv.at[m, me], y_dev),
+                remote(weights[m].at[:, cols(side, 1 - core)], wmate.at[m, 1], b_send.at[m, 1], wm_recv.at[m, 1], y_dev))
+
+    def forward_y(m):
+        return (remote(wbuf.at[m, x_dev], wbuf.at[m, x_dev], f_send.at[m, 0], w_recv.at[m, x_dev], y_dev),
+                remote(wmate.at[m, 0], wmate.at[m, 2], f_send.at[m, 1], wm_recv.at[m, 2], y_dev))
+
+    def to_mate(m, slot):
+        source = (x_dev, y_dev, dg_dev)[slot]
+        return remote(wmate.at[m, slot], wbuf.at[m, source], mf_send.at[m, slot], w_recv.at[m, source], mate)
+
+    def landed(m, source):
+        remote(wbuf.at[m, source], wbuf.at[m, source], m_send.at[m], w_recv.at[m, source], mate).wait_recv()
+
+    def landed_mate(m, slot):
+        to = wmate.at[m, slot]
+        remote(to, to, m_send.at[m], wm_recv.at[m, slot], mate).wait_recv()
+
+    def start(copies):
+        for copy in copies:
+            copy.start()
+
+    def n_copy(slot):
+        source, device = (0, 0, 0, 2)[slot], (mate, mate, x_dev, mate)[slot]
+        return remote(nbuf.at[source], nbuf.at[slot], n_send.at[slot], n_recv.at[slot], device)
+
+    def id_copy(slot, owner):
+        return remote(ids_hbm, ids_buf.at[owner], i_send.at[slot], i_recv.at[owner], others[slot])
+
+    def rows(piece):
+        return pl.ds(piece * part, part)
+
+    def wo_x(slot, source, piece, src):
+        return remote(src, wfull_hbm.at[source, rows(piece)], ox_send.at[slot], o_recv.at[source, piece], x_dev)
+
+    def wo_y(slot, source, piece, src):
+        return remote(src, wfull_hbm.at[source, rows(piece)], oy_send.at[slot], o_recv.at[source, piece], y_dev)
+
+    def wo_mate(order, source, piece, src):
+        return remote(src, wfull_hbm.at[source, rows(piece)], od_send.at[order, piece], o_recv.at[source, piece], mate)
+
+    def wo_landed(source, piece):
+        to = wfull_hbm.at[source, rows(piece)]
+        remote(to, to, od_send.at[0, 0], o_recv.at[source, piece], mate).wait_recv()
+
+    for slot in range(7):
+        id_copy(slot, me).start()
+    id_own = pltpu.make_async_copy(ids_hbm, ids_buf.at[me], i_own)
+    id_own.start()
+    start(over_x(0))
+    start(over_y(0))
+    for m in range(3):
+        local_w(m).start()
+        own_mate(m).start()
+    start(over_y(1))
+    wide = tok_ref[...].astype(jnp.float32)
+    nbuf[0] = (wide * lax.rsqrt(jnp.mean(wide * wide, axis=-1, keepdims=True) + EPS)).astype(jnp.bfloat16)
+    n_copy(2).start()
+    n_copy(1).start()
+    start(over_x(1))
+    start(over_x(2))
+    for piece in range(4):
+        wo_x(piece, me, piece, wo_hbm.at[rows(piece)]).start()
+    for piece in range(4):
+        wo_mate(0, me, piece, wo_hbm.at[rows(piece)]).start()
+    wo_own = pltpu.make_async_copy(wo_hbm, wfull_hbm.at[me], o_own)
+    wo_own.start()
+
+    id_own.wait()
+    for slot in range(7):
+        id_copy(slot, others[slot]).wait_recv()
+    order = lax.broadcasted_iota(jnp.int32, (tok, tok), 0) < lax.broadcasted_iota(jnp.int32, (tok, tok), 1)
+    earlier = jnp.where(order, 1.0, 0.0).astype(jnp.bfloat16)
+    experts = slots_ref.shape[1]
+    spot = lax.broadcasted_iota(jnp.int32, (experts, tok), 0)
+    local = experts // 2
+    wanted = jnp.where(spot < local, me * local + spot, (mate - 1) * local + spot)
+
+    def table(source, c):
+        count = jnp.zeros((experts, tok), jnp.float32)
+        for j in range(ids_buf.shape[1]):
+            count = count + jnp.where(ids_buf[source, j:j + 1, :] == wanted, 1.0, 0.0)
+        before = jnp.dot(count.astype(jnp.bfloat16), earlier, preferred_element_type=jnp.float32)
+        slots_ref[source] = jnp.where(count > 0.0, before, -1.0)
+        ids_ref[source] = ids_buf[source]
+        return c
+
+    lax.fori_loop(0, ids_buf.shape[0], table, 0)
+
+    def arrive_x(m):
+        landed(m, x_dev)
+        landed_mate(m, 0)
+        start(forward_y(m))
+        to_mate(m, 0).start()
+
+    def finish(m):
+        landed_mate(m, 1)
+        to_mate(m, 1).start()
+        landed_mate(m, 2)
+        to_mate(m, 2).start()
+        local_w(m).wait()
+        for source in (y_dev, dg_dev, mate, x_mate, yn * 2 + 1 - core, dg * 2 + 1 - core):
+            landed(m, source)
+
+    width = 256
+
+    def project(m):
+        def run(i, c):
+            slot, n = i // (group // width), lax.rem(i, group // width)
+            at = pl.ds(pl.multiple_of(n * width, width), width)
+            out = jnp.dot(nbuf[slot], wbuf[m, :, :, at].reshape(dim, width), preferred_element_type=jnp.float32)
+            qkv[m, slot, :, at] = out.astype(jnp.bfloat16)
+            return c
+
+        lax.fori_loop(0, seqs * (group // width), run, 0)
+
+    arrive_x(0)
+    start(over_y(2))
+    n_copy(2).wait_recv()
+    n_copy(3).start()
+    finish(0)
+    n_copy(1).wait_recv()
+    n_copy(3).wait_recv()
+    project(0)
+    arrive_x(1)
+    arrive_x(2)
+    for slot, piece in enumerate((3, 0, 1, 2)):
+        wo_y(slot, me, piece, wo_hbm.at[rows(piece)]).start()
+    finish(1)
+    project(1)
+    finish(2)
+    project(2)
+
+    scale = 128 ** -0.5
+    block = tok // 2
+    pairs = group // 256
+
+    def c_copy(slot, pair):
+        at = pl.ds(pl.multiple_of(pair * 256, 256), 256)
+        there = pl.ds(pl.multiple_of((2 * side + core) * group + pair * 256, 256), 256)
+        src, dst = cbuf.at[slot, :, at], ctx_hbm.at[:, there]
+        if slot == 0:
+            return pltpu.make_async_copy(src, dst, c_own.at[pair])
+        return remote(src, dst, c_send.at[slot - 1, pair], c_recv.at[slot - 1, pair], (mate, x_dev, x_mate)[slot - 1])
+
+    def heads(pair, carry):
+        def one_seq(slot, c):
+            for h in range(2):
+                at = pl.ds(pl.multiple_of(pair * 256 + h * 128, 128), 128)
+                keys, values = qkv[1, slot, :, at], qkv[2, slot, :, at]
+                for b in range(2):
+                    query = qkv[0, slot, b * block:(b + 1) * block, at]
+                    span = (b + 1) * block
+                    s = lax.dot_general(query, keys[:span], (((1,), (1,)), ((), ())), preferred_element_type=jnp.float32) * scale
+                    row = lax.broadcasted_iota(jnp.int32, (block, span), 0) + b * block
+                    s = jnp.where(row >= lax.broadcasted_iota(jnp.int32, (block, span), 1), s, -jnp.inf)
+                    e = jnp.exp(s - jnp.max(s, axis=-1, keepdims=True))
+                    p = (e * (1.0 / jnp.sum(e, axis=-1, keepdims=True))).astype(jnp.bfloat16)
+                    cbuf[slot, b * block:(b + 1) * block, at] = jnp.dot(p, values[:span], preferred_element_type=jnp.float32).astype(jnp.bfloat16)
+            return c
+
+        lax.fori_loop(0, seqs, one_seq, 0)
+        for slot in (2, 3, 1, 0):
+            c_copy(slot, pair).start()
+
+        @pl.when(pair == 1)
+        def _():
+            for piece in range(4):
+                wo_landed(x_dev, piece)
+                wo_mate(1, x_dev, piece, wfull_hbm.at[x_dev, rows(piece)]).start()
+                if piece < 3:
+                    wo_y(4 + piece, x_dev, piece, wfull_hbm.at[x_dev, rows(piece)]).start()
+
+        return carry
+
+    lax.fori_loop(0, pairs, heads, 0)
+    for piece in (3, 0, 1, 2):
+        wo_landed(y_dev, piece)
+        wo_mate(2, y_dev, piece, wfull_hbm.at[y_dev, rows(piece)]).start()
+        if piece == 3:
+            wo_x(4, y_dev, piece, wfull_hbm.at[y_dev, rows(piece)]).start()
+    for piece in (0, 1, 2, 3):
+        wo_landed(dg_dev, piece)
+        wo_mate(3, dg_dev, piece, wfull_hbm.at[dg_dev, rows(piece)]).start()
+    for slot in range(1, 4):
+        for pair in range(4):
+            at = pl.ds(pair * 256, 256)
+            remote(cbuf.at[0, :, at], ctx_hbm.at[:, at], c_send.at[slot - 1, pair], c_recv.at[slot - 1, pair], mate).wait_recv()
+    for source in (mate, x_mate, yn * 2 + 1 - core, dg * 2 + 1 - core):
+        for piece in range(4):
+            wo_landed(source, piece)
+    for slot in range(7):
+        id_copy(slot, me).wait_send()
+    for m in range(3):
+        own_mate(m).wait_send()
+        for copy in over_x(m) + over_y(m) + forward_y(m):
+            copy.wait_send()
+        for slot in range(3):
+            to_mate(m, slot).wait_send()
+    for slot in range(1, 4):
+        n_copy(slot).wait_send()
+    for pair in range(4):
+        c_copy(0, pair).wait()
+        for slot in range(1, 4):
+            c_copy(slot, pair).wait_send()
+    wo_own.wait()
+    for slot in range(5):
+        wo_x(slot, me, 0, wo_hbm.at[rows(0)]).wait_send()
+    for slot in range(7):
+        wo_y(slot, me, 0, wo_hbm.at[rows(0)]).wait_send()
+    for order in range(4):
+        for piece in range(4):
+            wo_mate(order, me, piece, wo_hbm.at[rows(piece)]).wait_send()
+
+
+def attend(tokens, ids, w_query, w_key, w_value, w_out):
+    tok, dim = tokens.shape
+    depth, width = w_query.shape
+    devices, group = 8, width // 4
+    dma = pltpu.SemaphoreType.DMA
+    any_spec = pl.BlockSpec(memory_space=pl.ANY)
+    return pl.pallas_call(
+        attend_kernel,
+        out_shape=(jax.ShapeDtypeStruct((tok, width), jnp.bfloat16), jax.ShapeDtypeStruct((devices,) + w_out.shape, jnp.bfloat16), jax.ShapeDtypeStruct((devices, 32, tok), jnp.float32), jax.ShapeDtypeStruct((devices,) + ids.shape, jnp.int32)),
+        in_specs=[pl.BlockSpec(memory_space=pltpu.VMEM)] + [any_spec] * 5,
+        out_specs=(any_spec, any_spec, pl.BlockSpec(memory_space=pltpu.VMEM), pl.BlockSpec(memory_space=pltpu.VMEM)),
+        scratch_shapes=[
+            pltpu.VMEM((devices,) + ids.shape, jnp.int32), dma((7,)), dma((devices,)), dma,
+            pltpu.VMEM((4, tok, dim), jnp.bfloat16),
+            pltpu.VMEM((3, devices, depth, group), jnp.bfloat16),
+            pltpu.VMEM((3, 3, depth, group), jnp.bfloat16),
+            pltpu.VMEM((3, 4, tok, group), jnp.bfloat16),
+            pltpu.VMEM((4, tok, group), jnp.bfloat16),
+            dma((3,)), dma((3, 2)), dma((3, 2)), dma((3, 2)), dma((3,)), dma((3, 3)), dma((3, devices)), dma((3, 3)),
+            dma((4,)), dma((4,)), dma((3, 4)), dma((3, 4)), dma((4,)),
+            dma((5,)), dma((7,)), dma((4, 4)), dma((devices, 4)), dma,
+        ],
+        compiler_params=pltpu.CompilerParams(collective_id=3, has_side_effects=True, vmem_limit_bytes=VMEM_MAX),
+        name='attend_heads',
+    )(tokens, ids, w_query, w_key, w_value, w_out)
+
+
 def spread_kernel(u_hbm, g_hbm, slot_ref, x_hbm, gall_hbm, ubuf, hbuf, xbuf, own_sem, gown_sem, out_sem, x_send, y_send, d_send, recv, g_send, g_recv):
     me, core, chip, xn, yn, dg = neighbours()
     mate = me + 1 - 2 * core
     tok = ubuf.shape[1]
     part = tok // 4
-    local_experts = slot_ref.shape[1]
+    local_experts = slot_ref.shape[1] // 2
     x_dev, y_dev, dg_dev = xn * 2 + core, yn * 2 + core, dg * 2 + core
     others = (x_dev, y_dev, mate, dg_dev, xn * 2 + 1 - core, yn * 2 + 1 - core, dg * 2 + 1 - core)
     greet(others)
@@ -137,7 +389,7 @@
         def _():
             out_copy(order, source).wait()
 
-        spot = lax.broadcasted_iota(jnp.int32, (CAP, tok), 0)
+        spot = lax.broadcasted_iota(jnp.int32, (CAP, tok), 0).astype(jnp.float32)
         for expert in range(local_experts):
             hit = slot_ref[source, expert:expert + 1, :] == spot
             hbuf[expert * CAP:(expert + 1) * CAP, :] = jnp.where(hit, 1.0, 0.0).astype(jnp.bfloat16)
@@ -172,7 +424,8 @@
 
 
 def spread(u, gates, slots):
-    devices, local_experts, tok = slots.shape
+    devices, pair_experts, tok = slots.shape
+    local_experts = pair_experts // 2
     dim = u.shape[1]
     return pl.pallas_call(
         spread_kernel,
@@ -468,26 +721,18 @@
         local_experts = w_one.shape[0]
         tok_count = seq_count * seq_len
         ids_t = expert_ids.reshape(tok_count, choices).T
-        all_ids = lax.all_gather(ids_t, 'ep', axis=0)
+        flat = tokens.reshape(tok_count, model_dim)
+        w_flat = [w.reshape(w.shape[0], -1) for w in (w_query, w_key, w_value)]
+        context, full_out, slot, all_ids = attend(flat, ids_t, *w_flat, w_out)
+        units = ((jnp.max(slot[:, :local_experts], axis=2).astype(jnp.int32) + UNIT) // UNIT).T.reshape(-1)
+        mixed = jnp.dot(context, full_out.reshape(-1, model_dim), preferred_element_type=jnp.float32)
+        hidden = (flat.astype(jnp.float32) + mixed).astype(jnp.bfloat16)
+        normed, gates = router_gates(hidden, w_router, ids_t)
+        x, all_gates = spread(normed, gates, slot)
         me = lax.axis_index('ep')
-        core = lax.rem(me, 2)
         local = jnp.arange(local_experts, dtype=jnp.int32)
-        wanted = jnp.concatenate([me * local_experts + local, (me + 1 - 2 * core) * local_experts + local])
+        wanted = jnp.concatenate([me * local_experts + local, (me + 1 - 2 * lax.rem(me, 2)) * local_experts + local])
         hit = all_ids[:, :, None, :] == wanted[None, None, :, None]
-        member = jnp.sum(hit.astype(jnp.int32), axis=1)
-        before = jnp.arange(tok_count)[:, None] < jnp.arange(tok_count)[None, :]
-        slot = jnp.einsum('set,tu->seu', member.astype(jnp.bfloat16), before.astype(jnp.bfloat16), preferred_element_type=jnp.float32)
-        slot = jnp.where(member > 0, slot, -1.0)
-        slots = slot[:, :local_experts].astype(jnp.int32)
-        units = ((jnp.sum(member[:, :local_experts], axis=2) + UNIT - 1) // UNIT).T.reshape(-1)
-
-        full_query = lax.all_gather(w_query, 'ep', axis=0, tiled=True)
-        full_key = lax.all_gather(w_key, 'ep', axis=0, tiled=True)
-        full_value = lax.all_gather(w_value, 'ep', axis=0, tiled=True)
-        full_out = lax.all_gather(w_out, 'ep', axis=0, tiled=True)
-        hidden = attention_layer(tokens, full_query, full_key, full_value, full_out).reshape(tok_count, model_dim)
-        normed, gates = router_gates(hidden, w_router, ids_t)
-        x, all_gates = spread(normed, gates, slots)
         gate = jnp.sum(jnp.where(hit, all_gates[:, :, None, :], 0.0), axis=1)
         tab = jnp.concatenate([slot, gate], axis=1)
         done = expert_ffn(units, x, w_one, w_three, w_two)

time: 723 us -> 604 us (0.84)
  waiting for transfers between devices: 234 us -> 0 us
  Pallas kernels: 331 us -> 564 us
  matrix products: 76.5 us -> 17.6 us
  other arithmetic: 44.4 us -> 7.44 us
  blocking collectives: 14.3 us -> 0 us
  between operations: 13.3 us -> 0.12 us
  local copies, waits for them, and re-layouts: 4.76 us -> 14.4 us
    all_gather x4 -> x0, waiting for transfers between devices: 232 us -> none  [the longest x1 72 us: local_layer(): full_key = lax.all_gather(w_key, 'ep', axis=0, tiled=True)]
    pallas_call x0 -> x1, Pallas kernels: none -> 228 us  [attend(): pl.pallas_call(attend_kernel, out_shape=(jax.ShapeDtypeStruct((tok, width...]
    dot_general x5 -> x1, matrix products: 73 us -> 14.1 us  [local_layer(): jnp.dot(context, full_out.reshape(-1, model_dim), preferred_element_type=...]
    sub x1 -> x0, other arithmetic: 34.1 us -> none  [attention_layer(): jax.nn.softmax(jnp.where(causal, scores, -jnp.inf), axis=-1)]
    all_gather x1 -> x0, blocking collectives: 14.3 us -> none  [local_layer(): all_ids = lax.all_gather(ids_t, 'ep', axis=0)]
  transfers between devices with their start and end apart: 4 -> 0, of which waited for: 4 -> 0; matrix products, arithmetic and copies ran while one was open for 14% -> 0% of each run, Pallas kernels for 0% -> 0%
where the time goes in v3:
time: 604 us
  Pallas kernels  564 us (93%)
  matrix products  17.6 us (3%)
  local copies, waits for them, and re-layouts  14.4 us (2%)
  other arithmetic  7.44 us (1%)
    pallas_call x1, Pallas kernels, attend(): pl.pallas_call(attend_kernel, out_shape=(jax.ShapeDtypeStruct((tok, width...  228 us
    pallas_call x1, Pallas kernels, combine(): pl.pallas_call(combine_kernel, out_shape=jax.ShapeDtypeStruct((tok, dim),...  158 us
    pallas_call x1, Pallas kernels, expert_ffn(): pl.pallas_call(ffn_kernel, out_shape=jax.ShapeDtypeStruct(x.shape, jnp.bf...  94.3 us
    pallas_call x1, Pallas kernels, spread(): pl.pallas_call(spread_kernel, out_shape=(jax.ShapeDtypeStruct((local_expe...  84 us
    dot_general x1, matrix products, local_layer(): jnp.dot(context, full_out.reshape(-1, model_dim), preferred_element_type=...  14.1 us

profile of v3, /device:TPU:0, one launch (start us, length us, event | category | flops | bytes accessed | tf_op | source)
XLA Modules:
  0.0 603.9 jit_solution(5969202981882907394)
XLA Ops:
  0.0 0.0 copy-start.1
  0.0 0.0 copy-start.2
  0.0 4.1 copy.23
  4.1 0.0 copy-done.1
  4.1 0.0 copy-done.2
  4.1 6.1 %copy_bitcast_fusion = (bf16[256,4096]{1,0:T(8,128)(2,1)}, bf16[256,4096]{1,0:T(8,128)(2,1)}) fusion(bf16[32,8,32,128]{3,2,1,0:T(8,128)(2,1)S(1)} %bitcast.42, bf16[32,8,32,128]{3,2,1,0:T(8,128)(2,1)S(1)} %bitcast.43), kind=kLoop, calls=%fused_computation.7 | loop fusion | bytes 8388608 | tf_op jit(solution)/shard_map/reshape | solution.py:725
  10.1 228.3 %attend_heads.1 = (bf16[512,4096]{1,0:T(8,128)(2,1)}, bf16[8,512,2048]{2,1,0:T(8,128)(2,1)}, f32[8,32,512]{2,1,0:T(8,128)}, s32[8,8,512]{2,1,0:T(8,128)}) custom-call(bf16[512,2048]{1,0:T(8,128)(2,1)} %bitcast.40, s32[8,512]{1,0:T(8,128)} %bitcast.44, bf16[256,4096]{1,0:T(8,128)(2,1)} %bitcast.38, bf16[256,4096]{1,0:T(8,128)(2,1)} %get-tuple-element.20.wk_hbm, ...), custom_call_target="tpu_custom_call" | custom-call | tf_op jit(solution)/shard_map/attend_heads/pallas_call | solution.py:294
  238.4 1.0 slice_reduce_fusion
  239.5 0.1 copy.15
  239.6 0.6 reshape.44.units_ref
  240.2 14.1 %fusion.2 = (f32[512]{0:T(512)S(1)}, bf16[512,2048]{1,0:T(8,128)(2,1)S(1)}) fusion(bf16[512,4096]{1,0:T(8,128)(2,1)} %get-tuple-element.12, bf16[4096,2048]{1,0:T(8,128)(2,1)} %bitcast.46, bf16[1,512,2048]{2,1,0:T(8,128)(2,1)} %param.10), kind=kOutput, calls=%fused_computation.4 | convolution fusion | flops 8596226048 | bytes 25167872 | tf_op jit(solution)/shard_map/dot_general | solution.py:728
  254.3 0.0 copy-start
  254.3 0.0 copy-start.3
  254.3 0.0 copy-start.4
  254.4 1.7 fusion.1.u_hbm
  256.1 0.2 copy-done
  256.3 0.0 copy-done.3
  256.3 3.5 fusion.4
  259.8 0.1 copy.16
  260.0 0.0 copy-done.4
  260.0 0.2 select_reduce_fusion.1
  260.3 0.6 fusion.5.g_hbm
  260.9 84.0 %spread_rows.1 = (bf16[16,8,64,2048]{3,2,1,0:T(8,128)(2,1)}, f32[8,8,512]{2,1,0:T(8,128)}) custom-call(bf16[512,2048]{1,0:T(8,128)(2,1)} %fusion.1.u_hbm, f32[8,512]{1,0:T(8,128)} %fusion.5.g_hbm, f32[8,32,512]{2,1,0:T(8,128)} %get-tuple-element.11.slot_ref), custom_call_target="tpu_custom_call" | custom-call | tf_op jit(solution)/shard_map/spread_rows/pallas_call | solution.py:430
  344.9 94.3 %expert_mlp.1.o_hbm = bf16[16,8,64,2048]{3,2,1,0:T(8,128)(2,1)} custom-call(s32[128]{0:T(128)} %reshape.44.units_ref, bf16[16,8,64,2048]{3,2,1,0:T(8,128)(2,1)} %get-tuple-element.14.x_ref, bf16[16,2048,768]{2,1,0:T(8,128)(2,1)} %w1_ref.1, bf16[16,2048,768]{2,1,0:T(8,128)(2,1)} %w3_ref.1, bf16[16,768,2048]{2,1,0:T(8,128)(2,1)} %w2_ref.1), custom_call_target="tpu_custom_call" | custom-call | tf_op jit(solution)/shard_map/expert_mlp/pallas_call | solution.py:497
  439.2 0.1 pad_add_fusion
  439.3 1.6 select_reduce_fusion
  440.9 2.1 pad_maximum_fusion.tab_hbm
  443.0 157.7 %combine_rows.1 = bf16[512,2048]{1,0:T(8,128)(2,1)} custom-call(bf16[16,8,64,2048]{3,2,1,0:T(8,128)(2,1)} %expert_mlp.1.o_hbm, f32[8,64,512]{2,1,0:T(8,128)} %pad_maximum_fusion.tab_hbm, bf16[512,2048]{1,0:T(8,128)(2,1)} %copy-done), custom_call_target="tpu_custom_call" | custom-call | tf_op jit(solution)/shard_map/combine_rows/pallas_call | solution.py:691
  600.7 3.2 copy.25
  (5 shorter events, 0.1 us)
Async XLA Ops:
  0.0 4.1 copy-start.1
  0.0 4.1 copy-start.2
  254.3 2.0 copy-start
  254.3 2.0 copy-start.3
  254.3 5.6 copy-start.4

commit v4 on v3

--- a/solution.py
+++ b/solution.py
@@ -11,6 +11,26 @@
 CAP = 64
 UNIT = 16
 VMEM_MAX = 67043328
+LANES = 128
+TILE = 256
+CORES = 2
+PARTS = 4
+ANY = pl.BlockSpec(memory_space=pl.ANY)
+WHOLE = pl.BlockSpec(memory_space=pltpu.VMEM)
+
+
+def strips(size, width):
+    return [slice(at, at + width) for at in range(0, size, width)]
+
+
+def start(copies):
+    for copy in copies:
+        copy.start()
+
+
+def finish_send(copies):
+    for copy in copies:
+        copy.wait_send()
 
 
 def rms_norm(vals):
@@ -48,12 +68,12 @@
     me, core, chip, xn, yn, dg = neighbours()
     side = lax.rem(chip, 2)
     mate = me + 1 - 2 * core
-    x_dev, y_dev, dg_dev, x_mate = xn * 2 + core, yn * 2 + core, dg * 2 + core, xn * 2 + 1 - core
+    x_dev, y_dev, dg_dev, x_mate = xn * CORES + core, yn * CORES + core, dg * CORES + core, xn * CORES + 1 - core
     weights = (wq_hbm, wk_hbm, wv_hbm)
     seqs, tok, dim = nbuf.shape
     group = wbuf.shape[3]
     part = tok // 4
-    others = (x_dev, y_dev, mate, x_mate, dg_dev, yn * 2 + 1 - core, dg * 2 + 1 - core)
+    others = (x_dev, y_dev, mate, x_mate, dg_dev, yn * CORES + 1 - core, dg * CORES + 1 - core)
     greet(others)
 
     def cols(on_side, on_core):
@@ -87,10 +107,6 @@
     def landed_mate(m, slot):
         to = wmate.at[m, slot]
         remote(to, to, m_send.at[m], wm_recv.at[m, slot], mate).wait_recv()
-
-    def start(copies):
-        for copy in copies:
-            copy.start()
 
     def n_copy(slot):
         source, device = (0, 0, 0, 2)[slot], (mate, mate, x_dev, mate)[slot]
@@ -131,9 +147,9 @@
     n_copy(1).start()
     start(over_x(1))
     start(over_x(2))
-    for piece in range(4):
+    for piece in range(PARTS):
         wo_x(piece, me, piece, wo_hbm.at[rows(piece)]).start()
-    for piece in range(4):
+    for piece in range(PARTS):
         wo_mate(0, me, piece, wo_hbm.at[rows(piece)]).start()
     wo_own = pltpu.make_async_copy(wo_hbm, wfull_hbm.at[me], o_own)
     wo_own.start()
@@ -171,7 +187,7 @@
         landed_mate(m, 2)
         to_mate(m, 2).start()
         local_w(m).wait()
-        for source in (y_dev, dg_dev, mate, x_mate, yn * 2 + 1 - core, dg * 2 + 1 - core):
+        for source in (y_dev, dg_dev, mate, x_mate, yn * CORES + 1 - core, dg * CORES + 1 - core):
             landed(m, source)
 
     width = 256
@@ -237,7 +253,7 @@
 
         @pl.when(pair == 1)
         def _():
-            for piece in range(4):
+            for piece in range(PARTS):
                 wo_landed(x_dev, piece)
                 wo_mate(1, x_dev, piece, wfull_hbm.at[x_dev, rows(piece)]).start()
                 if piece < 3:
@@ -255,11 +271,11 @@
         wo_landed(dg_dev, piece)
         wo_mate(3, dg_dev, piece, wfull_hbm.at[dg_dev, rows(piece)]).start()
     for slot in range(1, 4):
-        for pair in range(4):
+        for pair in range(PARTS):
             at = pl.ds(pair * 256, 256)
             remote(cbuf.at[0, :, at], ctx_hbm.at[:, at], c_send.at[slot - 1, pair], c_recv.at[slot - 1, pair], mate).wait_recv()
-    for source in (mate, x_mate, yn * 2 + 1 - core, dg * 2 + 1 - core):
-        for piece in range(4):
+    for source in (mate, x_mate, yn * CORES + 1 - core, dg * CORES + 1 - core):
+        for piece in range(PARTS):
             wo_landed(source, piece)
     for slot in range(7):
         id_copy(slot, me).wait_send()
@@ -271,7 +287,7 @@
             to_mate(m, slot).wait_send()
     for slot in range(1, 4):
         n_copy(slot).wait_send()
-    for pair in range(4):
+    for pair in range(PARTS):
         c_copy(0, pair).wait()
         for slot in range(1, 4):
             c_copy(slot, pair).wait_send()
@@ -280,8 +296,8 @@
         wo_x(slot, me, 0, wo_hbm.at[rows(0)]).wait_send()
     for slot in range(7):
         wo_y(slot, me, 0, wo_hbm.at[rows(0)]).wait_send()
-    for order in range(4):
-        for piece in range(4):
+    for order in range(PARTS):
+        for piece in range(PARTS):
             wo_mate(order, me, piece, wo_hbm.at[rows(piece)]).wait_send()
 
 
@@ -290,12 +306,11 @@
     depth, width = w_query.shape
     devices, group = 8, width // 4
     dma = pltpu.SemaphoreType.DMA
-    any_spec = pl.BlockSpec(memory_space=pl.ANY)
     return pl.pallas_call(
         attend_kernel,
         out_shape=(jax.ShapeDtypeStruct((tok, width), jnp.bfloat16), jax.ShapeDtypeStruct((devices,) + w_out.shape, jnp.bfloat16), jax.ShapeDtypeStruct((devices, 32, tok), jnp.float32), jax.ShapeDtypeStruct((devices,) + ids.shape, jnp.int32)),
-        in_specs=[pl.BlockSpec(memory_space=pltpu.VMEM)] + [any_spec] * 5,
-        out_specs=(any_spec, any_spec, pl.BlockSpec(memory_space=pltpu.VMEM), pl.BlockSpec(memory_space=pltpu.VMEM)),
+        in_specs=[WHOLE] + [ANY] * 5,
+        out_specs=(ANY, ANY, WHOLE, WHOLE),
         scratch_shapes=[
             pltpu.VMEM((devices,) + ids.shape, jnp.int32), dma((7,)), dma((devices,)), dma,
             pltpu.VMEM((4, tok, dim), jnp.bfloat16),
@@ -318,8 +333,8 @@
     tok = ubuf.shape[1]
     part = tok // 4
     local_experts = slot_ref.shape[1] // 2
-    x_dev, y_dev, dg_dev = xn * 2 + core, yn * 2 + core, dg * 2 + core
-    others = (x_dev, y_dev, mate, dg_dev, xn * 2 + 1 - core, yn * 2 + 1 - core, dg * 2 + 1 - core)
+    x_dev, y_dev, dg_dev = xn * CORES + core, yn * CORES + core, dg * CORES + core
+    others = (x_dev, y_dev, mate, dg_dev, xn * CORES + 1 - core, yn * CORES + 1 - core, dg * CORES + 1 - core)
     greet(others)
 
     def rows(piece):
@@ -341,10 +356,10 @@
     own.start()
     gown = pltpu.make_async_copy(g_hbm, gall_hbm.at[me], gown_sem)
     gown.start()
-    for slot in range(4):
+    for slot in range(PARTS):
         across_x(slot, me, slot, u_hbm.at[rows(slot)]).start()
         across_y(slot, me, (slot + 2) % 4, u_hbm.at[rows((slot + 2) % 4)]).start()
-    for piece in range(4):
+    for piece in range(PARTS):
         remote(u_hbm.at[rows(piece)], ubuf.at[me, rows(piece)], d_send.at[0, piece], recv.at[me, piece], mate).start()
     for slot, device in enumerate(others):
         remote(g_hbm, gall_hbm.at[me], g_send.at[slot], g_recv.at[me], device).start()
@@ -382,7 +397,7 @@
 
         @pl.when(odd == 1)
         def _():
-            for piece in range(4):
+            for piece in range(PARTS):
                 landed(source, piece)
 
         @pl.when(order >= 2)
@@ -409,14 +424,14 @@
     out_copy(0, me).wait()
     out_copy(1, me).wait()
     gown.wait()
-    for slot in range(4):
+    for slot in range(PARTS):
         across_x(slot, me, slot, u_hbm.at[rows(slot)]).wait_send()
         across_y(slot, me, slot, u_hbm.at[rows(slot)]).wait_send()
     for piece in (0, 1):
         across_y(4 + piece, x_dev, piece, ubuf.at[x_dev, rows(piece)]).wait_send()
         across_x(4 + piece, y_dev, piece + 2, ubuf.at[y_dev, rows(piece + 2)]).wait_send()
     for order, source in enumerate((me, x_dev, y_dev, dg_dev)):
-        for piece in range(4):
+        for piece in range(PARTS):
             pass_on(order, source, piece).wait_send()
     for slot, device in enumerate(others):
         remote(g_hbm, gall_hbm.at[me], g_send.at[slot], g_recv.at[me], device).wait_send()
@@ -430,8 +445,8 @@
     return pl.pallas_call(
         spread_kernel,
         out_shape=(jax.ShapeDtypeStruct((local_experts, devices, CAP, dim), jnp.bfloat16), jax.ShapeDtypeStruct((devices,) + gates.shape, jnp.float32)),
-        in_specs=[pl.BlockSpec(memory_space=pl.ANY), pl.BlockSpec(memory_space=pl.ANY), pl.BlockSpec(memory_space=pltpu.VMEM)],
-        out_specs=(pl.BlockSpec(memory_space=pl.ANY), pl.BlockSpec(memory_space=pl.ANY)),
+        in_specs=[ANY, ANY, WHOLE],
+        out_specs=(ANY, ANY),
         scratch_shapes=[
             pltpu.VMEM((devices, tok, dim), jnp.bfloat16),
             pltpu.VMEM((local_experts * CAP, tok), jnp.bfloat16),
@@ -445,104 +460,117 @@
     )(u, gates, slots)
 
 
-def ffn_kernel(units_ref, x_ref, w1_ref, w3_ref, w2_ref, o_ref, packed, middle, done):
+def ffn_kernel(units_ref, x_ref, w1_hbm, w3_hbm, w2_hbm, o_ref, packed, middle, done, w1_buf, w3_buf, w2_buf, w_sem):
     expert = pl.program_id(0)
+    last = pl.num_programs(0)
     devices = x_ref.shape[1]
-    tile = 128
+    depth = w1_buf.shape[0]
+    ahead = depth - 1
+
+    def fetch(e):
+        slot = lax.rem(e, depth)
+        moves = ((w1_hbm, w1_buf), (w3_hbm, w3_buf), (w2_hbm, w2_buf))
+        return [pltpu.make_async_copy(src.at[e], dst.at[slot], w_sem.at[slot, i]) for i, (src, dst) in enumerate(moves)]
+
+    @pl.when(expert == 0)
+    def _():
+        for e in range(ahead):
+            start(fetch(e))
+        packed[...] = jnp.zeros_like(packed)
+        done[...] = jnp.zeros_like(done)
+
+    @pl.when(expert + ahead < last)
+    def _():
+        start(fetch(expert + ahead))
+
+    begins, counts = [], [units_ref[expert * devices + source] * UNIT for source in range(devices)]
     total = 0
     for source in range(devices):
-        count = units_ref[expert * devices + source]
-
-        def pack(i, c, source=source, total=total):
-            packed[pl.ds(pl.multiple_of((total + i) * UNIT, UNIT), UNIT), :] = x_ref[0, source, pl.ds(pl.multiple_of(i * UNIT, UNIT), UNIT), :]
-            return c
-
-        lax.fori_loop(0, count, pack, 0)
-        total = total + count
-
-    def run(t, c):
-        rows = pl.ds(pl.multiple_of(t * tile, tile), tile)
-        for n in range(w1_ref.shape[2] // 256):
-            cols = slice(n * 256, (n + 1) * 256)
-            first = jnp.dot(packed[rows, :], w1_ref[0, :, cols], preferred_element_type=jnp.float32)
-            third = jnp.dot(packed[rows, :], w3_ref[0, :, cols], preferred_element_type=jnp.float32)
-            middle[:, cols] = (first * jax.nn.sigmoid(first) * third).astype(jnp.bfloat16)
-        for n in range(w2_ref.shape[2] // 512):
-            cols = slice(n * 512, (n + 1) * 512)
-            done[rows, cols] = jnp.dot(middle[...], w2_ref[0, :, cols], preferred_element_type=jnp.float32).astype(jnp.bfloat16)
+        begins.append(pl.multiple_of(total, UNIT))
+        packed[pl.ds(begins[-1], CAP), :] = x_ref[0, source]
+        total = total + counts[source]
+    for copy in fetch(expert):
+        copy.wait()
+    slot = lax.rem(expert, depth)
+    small, big = LANES, TILE
+
+    def run(begin, size):
+        rows = pl.ds(pl.multiple_of(begin, small), size)
+        for at in strips(w1_buf.shape[2], TILE):
+            first = jnp.dot(packed[rows, :], w1_buf[slot, :, at], preferred_element_type=jnp.float32)
+            third = jnp.dot(packed[rows, :], w3_buf[slot, :, at], preferred_element_type=jnp.float32)
+            middle[:size, at] = (first * jax.nn.sigmoid(first) * third).astype(jnp.bfloat16)
+        for at in strips(w2_buf.shape[2], 2 * TILE):
+            done[rows, at] = jnp.dot(middle[:size], w2_buf[slot, :, at], preferred_element_type=jnp.float32).astype(jnp.bfloat16)
+
+    full = (total + small - 1) // big
+
+    def run_big(t, c):
+        run(t * big, big)
         return c
 
-    lax.fori_loop(0, (total * UNIT + tile - 1) // tile, run, 0)
-    total = 0
+    lax.fori_loop(0, full, run_big, 0)
+
+    @pl.when(full * big < total)
+    def _():
+        run(full * big, small)
+
+    spot = lax.broadcasted_iota(jnp.int32, (CAP, o_ref.shape[3]), 0)
     for source in range(devices):
-        count = units_ref[expert * devices + source]
-
-        def unpack(i, c, source=source, total=total):
-            o_ref[0, source, pl.ds(pl.multiple_of(i * UNIT, UNIT), UNIT), :] = done[pl.ds(pl.multiple_of((total + i) * UNIT, UNIT), UNIT), :]
-            return c
-
-        def clear(i, c, source=source):
-            o_ref[0, source, pl.ds(pl.multiple_of(i * UNIT, UNIT), UNIT), :] = jnp.zeros((UNIT, o_ref.shape[3]), jnp.bfloat16)
-            return c
-
-        lax.fori_loop(0, count, unpack, 0)
-        lax.fori_loop(count, CAP // UNIT, clear, 0)
-        total = total + count
+        o_ref[0, source] = jnp.where(spot < counts[source], done[pl.ds(begins[source], CAP), :], jnp.zeros((), jnp.bfloat16))
 
 
 def expert_ffn(units, x, w_one, w_three, w_two):
     experts, devices, _, dim = x.shape
     mid = w_one.shape[2]
-    block = lambda *shape: pl.BlockSpec((1,) + shape, lambda e, units: (e,) + (0,) * len(shape))
+    depth = 3
+    block = pl.BlockSpec((1, devices, CAP, dim), lambda e, units: (e, 0, 0, 0))
+    ring = [pltpu.VMEM((depth,) + w.shape[1:], jnp.bfloat16) for w in (w_one, w_three, w_two)]
+    lines = pltpu.VMEM(((devices + 1) * CAP, dim), jnp.bfloat16)
     return pl.pallas_call(
         ffn_kernel,
         out_shape=jax.ShapeDtypeStruct(x.shape, jnp.bfloat16),
         grid_spec=pltpu.PrefetchScalarGridSpec(
             num_scalar_prefetch=1,
             grid=(experts,),
-            in_specs=[block(devices, CAP, dim), block(dim, mid), block(dim, mid), block(mid, dim)],
-            out_specs=block(devices, CAP, dim),
-            scratch_shapes=[pltpu.VMEM((devices * CAP, dim), jnp.bfloat16), pltpu.VMEM((128, mid), jnp.bfloat16), pltpu.VMEM((devices * CAP, dim), jnp.bfloat16)],
+            in_specs=[block] + [ANY] * 3,
+            out_specs=block,
+            scratch_shapes=[lines, pltpu.VMEM((TILE, mid), jnp.bfloat16), lines] + ring + [pltpu.SemaphoreType.DMA((depth, 3))],
         ),
         compiler_params=pltpu.CompilerParams(dimension_semantics=('arbitrary',), vmem_limit_bytes=VMEM_MAX),
         name='expert_mlp',
     )(units, x, w_one, w_three, w_two)
 
 
-def combine_kernel(o_hbm, tab_hbm, h_hbm, y_ref, own, mate_rows, tab, gate3, p_one, r_one, p_two, r_two, p_last, r_last, own_sem, tab_sem, h_sem, mate_send, mate_recv, one_send, one_recv, two_send, two_recv, last_send, last_recv):
+def combine_kernel(o_hbm, slots_ref, ids_ref, gates_ref, h_hbm, y_ref, own, mate_rows, gate_tab, gate3, p_one, r_one, p_two, r_two, p_last, r_last, own_sem, h_sem, mate_send, mate_recv, one_send, one_recv, two_send, two_recv, last_send, last_recv):
     me, core, chip, xn, yn, dg = neighbours()
-    mate = me + 1 - 2 * core
+    mate = me + 1 - CORES * core
     near = xn + core * (yn - xn)
     far = yn + core * (xn - yn)
-    near_dev, far_dev = near * 2 + core, far * 2 + core
+    near_dev, far_dev = near * CORES + core, far * CORES + core
     half = own.shape[3]
     rows_n = p_one.shape[1]
     experts = own.shape[1]
     greet((near_dev, far_dev, mate))
     my_cols = pl.ds(pl.multiple_of(core * half, half), half)
     mate_cols = pl.ds(pl.multiple_of((1 - core) * half, half), half)
-
-    def dest(i, first, second):
-        pair = i // 2
+    spot = lax.broadcasted_iota(jnp.int32, gate_tab.shape, 0)
+    wanted = jnp.where(spot < experts, me * experts + spot, (mate - 1) * experts + spot)
+
+    def dest(i, first, second, front):
+        pair, odd = i // CORES, lax.rem(i, CORES)
         base = jnp.where(pair == 0, dg, jnp.where(pair == 1, first, jnp.where(pair == 2, second, chip)))
-        return base
+        return base * CORES + jnp.where(pair < 3, odd, front + odd * (1 - CORES * front))
 
     def my_dest(i):
-        odd = lax.rem(i, 2)
-        return dest(i, near, far) * 2 + jnp.where(i < 6, odd, 1 - core + odd * (2 * core - 1))
-
-    def mate_dest(i):
-        odd = lax.rem(i, 2)
-        return dest(i, far, near) * 2 + jnp.where(i < 6, odd, core + odd * (1 - 2 * core))
+        return dest(i, near, far, 1 - core)
 
     def to_mate(i):
-        return remote(o_hbm.at[:, mate_dest(i), :, mate_cols], mate_rows.at[i], mate_send.at[i], mate_recv.at[i], mate)
+        return remote(o_hbm.at[:, dest(i, far, near, core), :, mate_cols], mate_rows.at[i], mate_send.at[i], mate_recv.at[i], mate)
 
     def own_copy(i):
-        return pltpu.make_async_copy(o_hbm.at[:, my_dest(i), :, my_cols], own.at[lax.rem(i, 2)], own_sem.at[lax.rem(i, 2)])
-
-    def tab_copy(i):
-        return pltpu.make_async_copy(tab_hbm.at[my_dest(i)], tab.at[lax.rem(i, 2)], tab_sem.at[lax.rem(i, 2)])
+        slot = lax.rem(i, CORES)
+        return pltpu.make_async_copy(o_hbm.at[:, my_dest(i), :, my_cols], own.at[slot], own_sem.at[slot])
 
     def one_copy(n):
         return remote(p_one.at[n], r_one.at[n], one_send.at[n], one_recv.at[n], near_dev)
@@ -554,161 +582,126 @@
         return remote(p_last.at[n], r_last.at[n], last_send.at[n], last_recv.at[n], mate)
 
     own_copy(0).start()
-    tab_copy(0).start()
     for i in range(8):
         to_mate(i).start()
     residual = pltpu.make_async_copy(h_hbm, y_ref, h_sem)
     residual.start()
 
     def open_dest(i):
+        gate = jnp.zeros(gate_tab.shape, jnp.float32)
+        target = my_dest(i)
+        for j in range(ids_ref.shape[1]):
+            gate = gate + jnp.where(ids_ref[target, j:j + 1, :] == wanted, gates_ref[target, j:j + 1, :], 0.0)
+        gate_tab[...] = gate
         own_copy(i).wait()
-        tab_copy(i).wait()
         to_mate(i).wait_recv()
 
         @pl.when(i < 7)
         def _():
             own_copy(i + 1).start()
-            tab_copy(i + 1).start()
 
     def weights(i, part):
-        slot = lax.rem(i, 2)
+        target = my_dest(i)
         cols = pl.ds(pl.multiple_of(part * rows_n, rows_n), rows_n)
-        spot = lax.broadcasted_iota(jnp.int32, (2 * CAP, rows_n), 0)
-        low = spot < CAP
-        place = (spot - jnp.where(low, 0, CAP)).astype(jnp.float32)
-        for pair in range(experts):
-            at = tab[slot, 2 * pair:2 * pair + 2, cols]
-            gate = tab[slot, 2 * experts + 2 * pair:2 * experts + 2 * pair + 2, cols]
-            hit = jnp.where(low, at[0:1], at[1:2]) == place
-            value = jnp.where(hit, jnp.where(low, gate[0:1], gate[1:2]), 0.0).T
-            top = value.astype(jnp.bfloat16)
-            rest = value - top.astype(jnp.float32)
-            mid = rest.astype(jnp.bfloat16)
-            low_part = (rest - mid.astype(jnp.float32)).astype(jnp.bfloat16)
-            where = slice(pair * 2 * CAP, (pair + 1) * 2 * CAP)
-            gate3[0:rows_n, where] = top
-            gate3[rows_n:2 * rows_n, where] = mid
-            gate3[2 * rows_n:3 * rows_n, where] = low_part
+        line = lax.broadcasted_iota(jnp.int32, (2 * CAP, rows_n), 0)
+        low = line < CAP
+        place = (line - jnp.where(low, 0, CAP)).astype(jnp.float32)
+        for pair, where in enumerate(strips(gate3.shape[1], 2 * CAP)):
+            one, two = slice(2 * pair, 2 * pair + 1), slice(2 * pair + 1, 2 * pair + 2)
+            hit = jnp.where(low, slots_ref[target, one, cols], slots_ref[target, two, cols]) == place
+            rest = jnp.where(hit, jnp.where(low, gate_tab[one, cols], gate_tab[two, cols]), 0.0).T
+            for rows in strips(gate3.shape[0], rows_n):
+                term = rest.astype(jnp.bfloat16)
+                gate3[rows, where] = term
+                rest = rest - term.astype(jnp.float32)
 
     def products(i, part, sink):
+        @pl.when(part == 0)
+        def _():
+            open_dest(i)
+
         weights(i, part)
-        slot = lax.rem(i, 2)
+        slot = lax.rem(i, CORES)
         depth = experts * CAP
-        width = 256
 
         def tile(n, c):
-            cols = pl.ds(pl.multiple_of(n * width, width), width)
-            mine = own[slot, :, :, cols].reshape(depth, width)
-            other = mate_rows[i, :, :, cols].reshape(depth, width)
+            cols = pl.ds(pl.multiple_of(n * TILE, TILE), TILE)
+            mine = own[slot, :, :, cols].reshape(depth, TILE)
+            other = mate_rows[i, :, :, cols].reshape(depth, TILE)
             out = jnp.dot(gate3[:, :depth], mine, preferred_element_type=jnp.float32) + jnp.dot(gate3[:, depth:], other, preferred_element_type=jnp.float32)
-            sink(cols, out[0:rows_n] + out[rows_n:2 * rows_n] + out[2 * rows_n:3 * rows_n])
+            sink[:, cols] = sum(out[rows] for rows in strips(out.shape[0], rows_n))
             return c
 
-        lax.fori_loop(0, half // width, tile, 0)
+        lax.fori_loop(0, half // TILE, tile, 0)
+
+    lead, pair_n, part_n = p_one.shape[0], p_two.shape[0], p_two.shape[0] // CORES
 
     def phase_one(step, c):
-        i, part = step // 2, lax.rem(step, 2)
-
-        @pl.when(part == 0)
-        def _():
-            open_dest(i)
-
-        def sink(cols, value):
-            p_one[step, :, cols] = value
-
-        products(i, part, sink)
+        products(step // part_n, lax.rem(step, part_n), p_one.at[step])
         one_copy(step).start()
         return c
 
-    lax.fori_loop(0, 8, phase_one, 0)
+    lax.fori_loop(0, lead, phase_one, 0)
 
     def phase_two(step, c):
-        i, part = 4 + step // 2, lax.rem(step, 2)
-
-        @pl.when(part == 0)
-        def _():
-            open_dest(i)
-
-        def sink(cols, value):
-            p_two[step, :, cols] = value
-
-        products(i, part, sink)
+        products(4 + step // part_n, lax.rem(step, part_n), p_two.at[step])
         one_copy(step).wait_recv()
         p_two[step] = p_two[step] + r_one[step]
         two_copy(step).start()
         return c
 
-    lax.fori_loop(0, 4, phase_two, 0)
+    lax.fori_loop(0, pair_n, phase_two, 0)
     residual.wait()
 
     def phase_three(step, c):
-        i, part = 6 + step // 2, lax.rem(step, 2)
-
-        @pl.when(part == 0)
-        def _():
-            open_dest(i)
-
-        def sink(cols, value):
-            p_last[step, :, cols] = value
-
-        products(i, part, sink)
-        target = jnp.where(step < 2, 1 - core, core)
-        n = target * 2 + part
-        one_copy(4 + n).wait_recv()
+        part = lax.rem(step, part_n)
+        products(6 + step // part_n, part, p_last.at[step])
+        n = jnp.where(step < part_n, 1 - core, core) * part_n + part
+        one_copy(pair_n + n).wait_recv()
         two_copy(n).wait_recv()
-        p_last[step] = p_last[step] + (r_one[4 + n] + r_two[n])
-
-        @pl.when(step < 2)
+        p_last[step] = p_last[step] + (r_one[pair_n + n] + r_two[n])
+
+        @pl.when(step < part_n)
         def _():
             last_copy(step).start()
 
-        @pl.when(step >= 2)
+        @pl.when(step >= part_n)
         def _():
             rows = pl.ds(pl.multiple_of(part * rows_n, rows_n), rows_n)
             y_ref[rows, my_cols] = (y_ref[rows, my_cols].astype(jnp.float32) + p_last[step]).astype(jnp.bfloat16)
 
         return c
 
-    lax.fori_loop(0, 4, phase_three, 0)
-    for n in range(2):
+    lax.fori_loop(0, pair_n, phase_three, 0)
+    for n in range(part_n):
         rows = pl.ds(n * rows_n, rows_n)
         last_copy(n).wait_recv()
         y_ref[rows, mate_cols] = (y_ref[rows, mate_cols].astype(jnp.float32) + r_last[n]).astype(jnp.bfloat16)
-    for n in range(8):
-        to_mate(n).wait_send()
-        one_copy(n).wait_send()
-    for n in range(4):
-        two_copy(n).wait_send()
-    for n in range(2):
-        last_copy(n).wait_send()
-
-
-def combine(done, tab, hidden):
+    finish_send(to_mate(n) for n in range(8))
+    finish_send(one_copy(n) for n in range(lead))
+    finish_send(two_copy(n) for n in range(pair_n))
+    finish_send(last_copy(n) for n in range(part_n))
+
+
+def combine(done, slots, ids, gates, hidden):
     experts, devices, _, dim = done.shape
     tok = hidden.shape[0]
-    half, part = dim // 2, tok // 2
+    half, part = dim // CORES, tok // PARTS
+    pair_n = CORES * PARTS
     dma = pltpu.SemaphoreType.DMA
+    floats = lambda n: pltpu.VMEM((n, part, half), jnp.float32)
+    rows = lambda n: pltpu.VMEM((n, experts, CAP, half), jnp.bfloat16)
+    sizes = [CORES * pair_n, CORES * pair_n, pair_n, pair_n, pair_n, PARTS]
+    sems = [dma((n,)) for n in (devices, devices, 2 * pair_n, 2 * pair_n, pair_n, pair_n, PARTS, PARTS)]
     return pl.pallas_call(
         combine_kernel,
         out_shape=jax.ShapeDtypeStruct((tok, dim), jnp.bfloat16),
-        in_specs=[pl.BlockSpec(memory_space=pl.ANY)] * 3,
-        out_specs=pl.BlockSpec(memory_space=pltpu.VMEM),
-        scratch_shapes=[
-            pltpu.VMEM((2, experts, CAP, half), jnp.bfloat16),
-            pltpu.VMEM((devices, experts, CAP, half), jnp.bfloat16),
-            pltpu.VMEM((2,) + tab.shape[1:], jnp.float32),
-            pltpu.VMEM((3 * part, 2 * experts * CAP), jnp.bfloat16),
-            pltpu.VMEM((8, part, half), jnp.float32),
-            pltpu.VMEM((8, part, half), jnp.float32),
-            pltpu.VMEM((4, part, half), jnp.float32),
-            pltpu.VMEM((4, part, half), jnp.float32),
-            pltpu.VMEM((4, part, half), jnp.float32),
-            pltpu.VMEM((2, part, half), jnp.float32),
-            dma((2,)), dma((2,)), dma, dma((8,)), dma((8,)), dma((8,)), dma((8,)), dma((4,)), dma((4,)), dma((2,)), dma((2,)),
-        ],
+        in_specs=[ANY, WHOLE, WHOLE, WHOLE, ANY],
+        out_specs=WHOLE,
+        scratch_shapes=[rows(CORES), rows(devices), pltpu.VMEM(slots.shape[1:], jnp.float32), pltpu.VMEM((3 * part, CORES * experts * CAP), jnp.bfloat16)] + [floats(n) for n in sizes] + [dma((CORES,)), dma] + sems,
         compiler_params=pltpu.CompilerParams(collective_id=2, has_side_effects=True, vmem_limit_bytes=VMEM_MAX),
         name='combine_rows',
-    )(done, tab, hidden)
+    )(done, slots, ids, gates, hidden)
 
 
 def solution(mesh):
@@ -729,14 +722,8 @@
         hidden = (flat.astype(jnp.float32) + mixed).astype(jnp.bfloat16)
         normed, gates = router_gates(hidden, w_router, ids_t)
         x, all_gates = spread(normed, gates, slot)
-        me = lax.axis_index('ep')
-        local = jnp.arange(local_experts, dtype=jnp.int32)
-        wanted = jnp.concatenate([me * local_experts + local, (me + 1 - 2 * lax.rem(me, 2)) * local_experts + local])
-        hit = all_ids[:, :, None, :] == wanted[None, None, :, None]
-        gate = jnp.sum(jnp.where(hit, all_gates[:, :, None, :], 0.0), axis=1)
-        tab = jnp.concatenate([slot, gate], axis=1)
         done = expert_ffn(units, x, w_one, w_three, w_two)
-        layer_out = combine(done, tab, hidden)
+        layer_out = combine(done, slot, all_ids, all_gates, hidden)
         return layer_out.reshape(seq_count, seq_len, model_dim)
 
     return jax.shard_map(local_layer, mesh=mesh, in_specs=(tok_spec, row_spec, row_spec, row_spec, row_spec, P(), row_spec, row_spec, row_spec, tok_spec), out_specs=tok_spec, check_vma=False)

time: 604 us -> 583 us (0.965)
  Pallas kernels: 564 us -> 547 us
    pallas_call x1, Pallas kernels: 94.3 us -> 75.8 us  [expert_ffn(): pl.pallas_call(ffn_kernel, out_shape=jax.ShapeDtypeStruct(x.shape, jnp.bf...]
where the time goes in v4:
time: 583 us; the launch traced here: 582 us
  Pallas kernels  547 us (94%)
  matrix products  17.7 us (3%)
  local copies, waits for them, and re-layouts  14.4 us (2%)
    pallas_call x1, Pallas kernels, attend(): pl.pallas_call(attend_kernel, out_shape=(jax.ShapeDtypeStruct((tok, width...  228 us
    pallas_call x1, Pallas kernels, combine(): pl.pallas_call(combine_kernel, out_shape=jax.ShapeDtypeStruct((tok, dim),...  159 us
    pallas_call x1, Pallas kernels, spread(): pl.pallas_call(spread_kernel, out_shape=(jax.ShapeDtypeStruct((local_expe...  84 us
    pallas_call x1, Pallas kernels, expert_ffn(): pl.pallas_call(ffn_kernel, out_shape=jax.ShapeDtypeStruct(x.shape, jnp.bf...  75.8 us
    dot_general x1, matrix products, local_layer(): jnp.dot(context, full_out.reshape(-1, model_dim), preferred_element_type=...  14.3 us

profile of v4, /device:TPU:0, one launch (start us, length us, event | category | flops | bytes accessed | tf_op | source)
XLA Modules:
  0.0 581.9 jit_solution(557596246311560448)
XLA Ops:
  0.0 0.0 copy-start.2
  0.0 0.0 copy-start.3
  0.0 4.1 copy.23
  4.1 0.0 copy-done.2
  4.1 0.0 copy-done.3
  4.1 6.1 %copy_bitcast_fusion = (bf16[256,4096]{1,0:T(8,128)(2,1)}, bf16[256,4096]{1,0:T(8,128)(2,1)}) fusion(bf16[32,8,32,128]{3,2,1,0:T(8,128)(2,1)S(1)} %bitcast.42, bf16[32,8,32,128]{3,2,1,0:T(8,128)(2,1)S(1)} %bitcast.43), kind=kLoop, calls=%fused_computation.6 | loop fusion | bytes 8388608 | tf_op jit(solution)/shard_map/reshape | solution.py:718
  10.1 228.3 %attend_heads.1 = (bf16[512,4096]{1,0:T(8,128)(2,1)}, bf16[8,512,2048]{2,1,0:T(8,128)(2,1)}, f32[8,32,512]{2,1,0:T(8,128)}, s32[8,8,512]{2,1,0:T(8,128)}) custom-call(bf16[512,2048]{1,0:T(8,128)(2,1)} %bitcast.40, s32[8,512]{1,0:T(8,128)} %bitcast.44, bf16[256,4096]{1,0:T(8,128)(2,1)} %bitcast.38, bf16[256,4096]{1,0:T(8,128)(2,1)} %get-tuple-element.20.wk_hbm, ...), custom_call_target="tpu_custom_call" | custom-call | tf_op jit(solution)/shard_map/attend_heads/pallas_call | solution.py:309
  238.4 0.0 copy-start.1
  238.4 0.0 copy-start.4
  238.5 14.3 %fusion.2 = (f32[512]{0:T(512)S(1)}, bf16[512,2048]{1,0:T(8,128)(2,1)S(1)}) fusion(bf16[512,4096]{1,0:T(8,128)(2,1)} %get-tuple-element.12, bf16[4096,2048]{1,0:T(8,128)(2,1)} %bitcast.46, bf16[1,512,2048]{2,1,0:T(8,128)(2,1)} %param.10), kind=kOutput, calls=%fused_computation.4 | convolution fusion | flops 8596226048 | bytes 25167872 | tf_op jit(solution)/shard_map/dot_general | solution.py:721
  252.7 0.0 copy-start
  252.7 0.0 copy-done.1
  252.8 0.0 copy-start.5
  252.8 0.1 slice_reduce_fusion
  252.9 0.1 copy.15
  253.0 0.8 reshape.41.units_ref
  253.8 0.0 copy-done.4
  253.8 3.5 fusion.4
  257.3 0.1 copy.16
  257.4 0.0 copy-done.5
  257.4 0.2 select_reduce_fusion
  257.7 0.6 fusion.5.g_hbm
  258.3 0.0 copy-done
  258.4 1.7 fusion.1.u_hbm
  260.1 84.0 %spread_rows.1 = (bf16[16,8,64,2048]{3,2,1,0:T(8,128)(2,1)}, f32[8,8,512]{2,1,0:T(8,128)}) custom-call(bf16[512,2048]{1,0:T(8,128)(2,1)} %fusion.1.u_hbm, f32[8,512]{1,0:T(8,128)} %fusion.5.g_hbm, f32[8,32,512]{2,1,0:T(8,128)} %get-tuple-element.11.slot_ref.slots_ref), custom_call_target="tpu_custom_call" | custom-call | tf_op jit(solution)/shard_map/spread_rows/pallas_call | solution.py:445
  344.1 75.8 %expert_mlp.1.o_hbm = bf16[16,8,64,2048]{3,2,1,0:T(8,128)(2,1)} custom-call(s32[128]{0:T(128)} %reshape.41.units_ref, bf16[16,8,64,2048]{3,2,1,0:T(8,128)(2,1)} %get-tuple-element.14.x_ref, bf16[16,2048,768]{2,1,0:T(8,128)(2,1)} %w1_hbm.1, bf16[16,2048,768]{2,1,0:T(8,128)(2,1)} %w3_hbm.1, bf16[16,768,2048]{2,1,0:T(8,128)(2,1)} %w2_hbm.1), custom_call_target="tpu_custom_call" | custom-call | tf_op jit(solution)/shard_map/expert_mlp/pallas_call | solution.py:530
  419.9 158.9 %combine_rows.1 = bf16[512,2048]{1,0:T(8,128)(2,1)} custom-call(bf16[16,8,64,2048]{3,2,1,0:T(8,128)(2,1)} %expert_mlp.1.o_hbm, f32[8,32,512]{2,1,0:T(8,128)} %get-tuple-element.11.slot_ref.slots_ref, s32[8,8,512]{2,1,0:T(8,128)} %get-tuple-element.15.ids_ref, f32[8,8,512]{2,1,0:T(8,128)} %get-tuple-element.16.gates_ref, bf16[512,2048]{1,0:T(8,128)(2,1)} %copy-done), custom_call_target="tpu_custom_call" | custom-call | tf_op jit(solution)/shard_map/combine_rows/pallas_call | solution.py:696
  578.8 3.2 copy.25
  (4 shorter events, 0.1 us)
Async XLA Ops:
  0.0 4.1 copy-start.2
  0.0 4.1 copy-start.3
  238.4 14.3 %copy-start.1 = (f32[8,32,512]{2,1,0:T(8,128)S(1)}, f32[8,32,512]{2,1,0:T(8,128)}, u32[]{:S(2)}) copy-start(f32[8,32,512]{2,1,0:T(8,128)} %get-tuple-element.11.slot_ref.slots_ref) | copy-start | bytes 1572868
  238.4 15.4 %copy-start.4 = (f32[2048,128]{1,0:T(8,128)S(1)}, f32[2048,128]{1,0:T(8,128)}, u32[]{:S(2)}) copy-start(f32[2048,128]{1,0:T(8,128)} %param.15) | copy-start | bytes 3145732
  252.7 5.6 copy-start
  252.8 4.7 copy-start.5

commit v5 on v4

--- a/solution.py
+++ b/solution.py
@@ -33,19 +33,6 @@
         copy.wait_send()
 
 
-def rms_norm(vals):
-    wide = vals.astype(jnp.float32)
-    return wide * lax.rsqrt(jnp.mean(wide * wide, axis=-1, keepdims=True) + EPS)
-
-
-def router_gates(hidden, w_router, ids_t):
-    normed = rms_norm(hidden)
-    logits = jnp.einsum('td,de->et', normed, w_router, precision=lax.Precision.HIGHEST, preferred_element_type=jnp.float32)
-    hit = ids_t[:, None, :] == jnp.arange(w_router.shape[1], dtype=jnp.int32)[None, :, None]
-    chosen = jnp.sum(jnp.where(hit, logits[None], 0.0), axis=1)
-    return normed.astype(jnp.bfloat16), jax.nn.softmax(chosen, axis=0)
-
-
 def neighbours():
     me = lax.axis_index('ep')
     core, chip = lax.rem(me, 2), me // 2
@@ -64,7 +51,7 @@
     return pltpu.make_async_remote_copy(src_ref=src, dst_ref=dst, send_sem=send_sem, recv_sem=recv_sem, device_id={'ep': device}, device_id_type=pl.DeviceIdType.MESH)
 
 
-def attend_kernel(tok_ref, ids_hbm, wq_hbm, wk_hbm, wv_hbm, wo_hbm, ctx_hbm, wfull_hbm, slots_ref, ids_ref, ids_buf, i_send, i_recv, i_own, nbuf, wbuf, wmate, qkv, cbuf, loc_sem, a_send, b_send, f_send, m_send, mf_send, w_recv, wm_recv, n_send, n_recv, c_send, c_recv, c_own, ox_send, oy_send, od_send, o_recv, o_own):
+def attend_kernel(tok_ref, ids_hbm, wq_hbm, wk_hbm, wv_hbm, wo_hbm, h_hbm, u_hbm, wfull_hbm, slots_ref, ids_ref, ctx, total, out_sem, ring_sem, ids_buf, i_send, i_recv, i_own, nbuf, wbuf, wmate, qkv, cbuf, loc_sem, a_send, b_send, f_send, m_send, mf_send, w_recv, wm_recv, n_send, n_recv, c_send, c_recv, c_own, ox_send, oy_send, od_send, o_recv, o_own):
     me, core, chip, xn, yn, dg = neighbours()
     side = lax.rem(chip, 2)
     mate = me + 1 - 2 * core
@@ -226,7 +213,7 @@
     def c_copy(slot, pair):
         at = pl.ds(pl.multiple_of(pair * 256, 256), 256)
         there = pl.ds(pl.multiple_of((2 * side + core) * group + pair * 256, 256), 256)
-        src, dst = cbuf.at[slot, :, at], ctx_hbm.at[:, there]
+        src, dst = cbuf.at[slot, :, at], ctx.at[:, there]
         if slot == 0:
             return pltpu.make_async_copy(src, dst, c_own.at[pair])
         return remote(src, dst, c_send.at[slot - 1, pair], c_recv.at[slot - 1, pair], (mate, x_dev, x_mate)[slot - 1])
@@ -262,21 +249,58 @@
         return carry
 
     lax.fori_loop(0, pairs, heads, 0)
+    finish_send(n_copy(slot) for slot in range(1, PARTS))
+    total[...] = tok_ref[...].astype(jnp.float32)
     for piece in (3, 0, 1, 2):
         wo_landed(y_dev, piece)
         wo_mate(2, y_dev, piece, wfull_hbm.at[y_dev, rows(piece)]).start()
         if piece == 3:
             wo_x(4, y_dev, piece, wfull_hbm.at[y_dev, rows(piece)]).start()
-    for piece in (0, 1, 2, 3):
-        wo_landed(dg_dev, piece)
-        wo_mate(3, dg_dev, piece, wfull_hbm.at[dg_dev, rows(piece)]).start()
-    for slot in range(1, 4):
-        for pair in range(PARTS):
-            at = pl.ds(pair * 256, 256)
-            remote(cbuf.at[0, :, at], ctx_hbm.at[:, at], c_send.at[slot - 1, pair], c_recv.at[slot - 1, pair], mate).wait_recv()
-    for source in (mate, x_mate, yn * CORES + 1 - core, dg * CORES + 1 - core):
-        for piece in range(PARTS):
-            wo_landed(source, piece)
+    for slot in range(1, PARTS):
+        for at in strips(group, TILE):
+            remote(cbuf.at[0, :, at], ctx.at[:, at], c_send.at[0, 0], c_recv.at[slot - 1, at.start // TILE], mate).wait_recv()
+    for pair in range(PARTS):
+        c_copy(0, pair).wait()
+    wo_own.wait()
+    order = (me, x_dev, y_dev, mate, x_mate, yn * CORES + 1 - core, dg_dev, dg * CORES + 1 - core)
+
+    def load(step):
+        slot = step % CORES
+        return pltpu.make_async_copy(wfull_hbm.at[order[step]], nbuf.at[CORES + slot], ring_sem.at[slot])
+
+    def ready(step):
+        if step == 6:
+            for piece in range(PARTS):
+                wo_landed(dg_dev, piece)
+                wo_mate(3, dg_dev, piece, wfull_hbm.at[dg_dev, rows(piece)]).start()
+        elif step > 2:
+            for piece in range(PARTS):
+                wo_landed(order[step], piece)
+        load(step).start()
+
+    ready(0)
+    for step, source in enumerate(order):
+        early = step + 1 < 6
+        if early:
+            ready(step + 1)
+        load(step).wait()
+        heads_at = pl.ds(pl.multiple_of(source * wo_hbm.shape[0], wo_hbm.shape[0]), wo_hbm.shape[0])
+
+        def add(n, c, slot=step % CORES, heads_at=heads_at):
+            at = pl.ds(pl.multiple_of(n * TILE, TILE), TILE)
+            total[:, at] += jnp.dot(ctx[:, heads_at], nbuf[CORES + slot, :, at], preferred_element_type=jnp.float32)
+            return c
+
+        lax.fori_loop(0, dim // TILE, add, 0)
+        if not early and step + 1 < len(order):
+            ready(step + 1)
+    nbuf[0] = total[...].astype(jnp.bfloat16)
+    h_copy = pltpu.make_async_copy(nbuf.at[0], h_hbm, out_sem.at[0])
+    h_copy.start()
+    wide = nbuf[0].astype(jnp.float32)
+    nbuf[1] = (wide * lax.rsqrt(jnp.mean(wide * wide, axis=-1, keepdims=True) + EPS)).astype(jnp.bfloat16)
+    u_copy = pltpu.make_async_copy(nbuf.at[1], u_hbm, out_sem.at[1])
+    u_copy.start()
     for slot in range(7):
         id_copy(slot, me).wait_send()
     for m in range(3):
@@ -285,13 +309,10 @@
             copy.wait_send()
         for slot in range(3):
             to_mate(m, slot).wait_send()
-    for slot in range(1, 4):
-        n_copy(slot).wait_send()
     for pair in range(PARTS):
-        c_copy(0, pair).wait()
-        for slot in range(1, 4):
-            c_copy(slot, pair).wait_send()
-    wo_own.wait()
+        finish_send(c_copy(slot, pair) for slot in range(1, PARTS))
+    h_copy.wait()
+    u_copy.wait()
     for slot in range(5):
         wo_x(slot, me, 0, wo_hbm.at[rows(0)]).wait_send()
     for slot in range(7):
@@ -308,10 +329,11 @@
     dma = pltpu.SemaphoreType.DMA
     return pl.pallas_call(
         attend_kernel,
-        out_shape=(jax.ShapeDtypeStruct((tok, width), jnp.bfloat16), jax.ShapeDtypeStruct((devices,) + w_out.shape, jnp.bfloat16), jax.ShapeDtypeStruct((devices, 32, tok), jnp.float32), jax.ShapeDtypeStruct((devices,) + ids.shape, jnp.int32)),
+        out_shape=(jax.ShapeDtypeStruct((tok, dim), jnp.bfloat16), jax.ShapeDtypeStruct((tok, dim), jnp.bfloat16), jax.ShapeDtypeStruct((devices,) + w_out.shape, jnp.bfloat16), jax.ShapeDtypeStruct((devices, 32, tok), jnp.float32), jax.ShapeDtypeStruct((devices,) + ids.shape, jnp.int32)),
         in_specs=[WHOLE] + [ANY] * 5,
-        out_specs=(ANY, ANY, WHOLE, WHOLE),
+        out_specs=(ANY, ANY, ANY, WHOLE, WHOLE),
         scratch_shapes=[
+            pltpu.VMEM((tok, width), jnp.bfloat16), pltpu.VMEM((tok, dim), jnp.float32), dma((2,)), dma((2,)),
             pltpu.VMEM((devices,) + ids.shape, jnp.int32), dma((7,)), dma((devices,)), dma,
             pltpu.VMEM((4, tok, dim), jnp.bfloat16),
             pltpu.VMEM((3, devices, depth, group), jnp.bfloat16),
@@ -327,7 +349,7 @@
     )(tokens, ids, w_query, w_key, w_value, w_out)
 
 
-def spread_kernel(u_hbm, g_hbm, slot_ref, x_hbm, gall_hbm, ubuf, hbuf, xbuf, own_sem, gown_sem, out_sem, x_send, y_send, d_send, recv, g_send, g_recv):
+def spread_kernel(u_hbm, h_ref, router_ref, ids_ref, slot_ref, x_hbm, gall_hbm, g_own, ubuf, hbuf, xbuf, own_sem, gown_sem, out_sem, x_send, y_send, d_send, recv, g_send, g_recv):
     me, core, chip, xn, yn, dg = neighbours()
     mate = me + 1 - 2 * core
     tok = ubuf.shape[1]
@@ -354,15 +376,24 @@
 
     own = pltpu.make_async_copy(u_hbm, ubuf.at[me], own_sem)
     own.start()
-    gown = pltpu.make_async_copy(g_hbm, gall_hbm.at[me], gown_sem)
-    gown.start()
     for slot in range(PARTS):
         across_x(slot, me, slot, u_hbm.at[rows(slot)]).start()
         across_y(slot, me, (slot + 2) % 4, u_hbm.at[rows((slot + 2) % 4)]).start()
     for piece in range(PARTS):
         remote(u_hbm.at[rows(piece)], ubuf.at[me, rows(piece)], d_send.at[0, piece], recv.at[me, piece], mate).start()
+    wide = h_ref[...].astype(jnp.float32)
+    wide = wide * lax.rsqrt(jnp.mean(wide * wide, axis=-1, keepdims=True) + EPS)
+    logits = jnp.dot(wide, router_ref[...], precision=lax.Precision.HIGHEST, preferred_element_type=jnp.float32).T
+    expert_at = lax.broadcasted_iota(jnp.int32, logits.shape, 0)
+    for j in range(g_own.shape[0]):
+        g_own[j:j + 1, :] = jnp.sum(jnp.where(ids_ref[j:j + 1, :] == expert_at, logits, 0.0), axis=0, keepdims=True)
+    chosen = g_own[...]
+    chosen = jnp.exp(chosen - jnp.max(chosen, axis=0, keepdims=True))
+    g_own[...] = chosen / jnp.sum(chosen, axis=0, keepdims=True)
+    gown = pltpu.make_async_copy(g_own, gall_hbm.at[me], gown_sem)
+    gown.start()
     for slot, device in enumerate(others):
-        remote(g_hbm, gall_hbm.at[me], g_send.at[slot], g_recv.at[me], device).start()
+        remote(g_own, gall_hbm.at[me], g_send.at[slot], g_recv.at[me], device).start()
     own.wait()
 
     def out_copy(order, source):
@@ -434,20 +465,21 @@
         for piece in range(PARTS):
             pass_on(order, source, piece).wait_send()
     for slot, device in enumerate(others):
-        remote(g_hbm, gall_hbm.at[me], g_send.at[slot], g_recv.at[me], device).wait_send()
-        remote(g_hbm, gall_hbm.at[device], g_send.at[slot], g_recv.at[device], device).wait_recv()
-
-
-def spread(u, gates, slots):
+        remote(g_own, gall_hbm.at[me], g_send.at[slot], g_recv.at[me], device).wait_send()
+        remote(g_own, gall_hbm.at[device], g_send.at[slot], g_recv.at[device], device).wait_recv()
+
+
+def spread(u, hidden, w_router, ids, slots):
     devices, pair_experts, tok = slots.shape
     local_experts = pair_experts // 2
     dim = u.shape[1]
     return pl.pallas_call(
         spread_kernel,
-        out_shape=(jax.ShapeDtypeStruct((local_experts, devices, CAP, dim), jnp.bfloat16), jax.ShapeDtypeStruct((devices,) + gates.shape, jnp.float32)),
-        in_specs=[ANY, ANY, WHOLE],
+        out_shape=(jax.ShapeDtypeStruct((local_experts, devices, CAP, dim), jnp.bfloat16), jax.ShapeDtypeStruct((devices,) + ids.shape, jnp.float32)),
+        in_specs=[ANY, WHOLE, WHOLE, WHOLE, WHOLE],
         out_specs=(ANY, ANY),
         scratch_shapes=[
+            pltpu.VMEM(ids.shape, jnp.float32),
             pltpu.VMEM((devices, tok, dim), jnp.bfloat16),
             pltpu.VMEM((local_experts * CAP, tok), jnp.bfloat16),
             pltpu.VMEM((2, local_experts, CAP, dim), jnp.bfloat16),
@@ -457,7 +489,7 @@
         ],
         compiler_params=pltpu.CompilerParams(collective_id=1, has_side_effects=True, vmem_limit_bytes=VMEM_MAX),
         name='spread_rows',
-    )(u, gates, slots)
+    )(u, hidden, w_router, ids, slots)
 
 
 def ffn_kernel(units_ref, x_ref, w1_hbm, w3_hbm, w2_hbm, o_ref, packed, middle, done, w1_buf, w3_buf, w2_buf, w_sem):
@@ -716,12 +748,9 @@
         ids_t = expert_ids.reshape(tok_count, choices).T
         flat = tokens.reshape(tok_count, model_dim)
         w_flat = [w.reshape(w.shape[0], -1) for w in (w_query, w_key, w_value)]
-        context, full_out, slot, all_ids = attend(flat, ids_t, *w_flat, w_out)
+        hidden, normed, _, slot, all_ids = attend(flat, ids_t, *w_flat, w_out)
         units = ((jnp.max(slot[:, :local_experts], axis=2).astype(jnp.int32) + UNIT) // UNIT).T.reshape(-1)
-        mixed = jnp.dot(context, full_out.reshape(-1, model_dim), preferred_element_type=jnp.float32)
-        hidden = (flat.astype(jnp.float32) + mixed).astype(jnp.bfloat16)
-        normed, gates = router_gates(hidden, w_router, ids_t)
-        x, all_gates = spread(normed, gates, slot)
+        x, all_gates = spread(normed, hidden, w_router, ids_t, slot)
         done = expert_ffn(units, x, w_one, w_three, w_two)
         layer_out = combine(done, slot, all_ids, all_gates, hidden)
         return layer_out.reshape(seq_count, seq_len, model_dim)

time: 583 us -> 581 us (level)
  Pallas kernels: 547 us -> 568 us
  matrix products: 17.7 us -> 0 us
    dot_general x2 -> x0, matrix products: 17.7 us -> none  [the longest x1 14.3 us: local_layer(): jnp.dot(context, full_out.reshape(-1, model_dim), preferred_element_type=...]
    pallas_call x1, Pallas kernels: 228 us -> 244 us  [attend(): pl.pallas_call(attend_kernel, out_shape=(jax.ShapeDtypeStruct((tok, dim),...]
    pallas_call x1, Pallas kernels: 159 us -> 166 us  [combine(): pl.pallas_call(combine_kernel, out_shape=jax.ShapeDtypeStruct((tok, dim),...]
where the time goes in v5:
time: 581 us; the launch traced here: 583 us
  Pallas kernels  568 us (98%)
  local copies, waits for them, and re-layouts  14 us (2%)
    pallas_call x1, Pallas kernels, attend(): pl.pallas_call(attend_kernel, out_shape=(jax.ShapeDtypeStruct((tok, dim),...  244 us
    pallas_call x1, Pallas kernels, combine(): pl.pallas_call(combine_kernel, out_shape=jax.ShapeDtypeStruct((tok, dim),...  166 us
    pallas_call x1, Pallas kernels, spread(): pl.pallas_call(spread_kernel, out_shape=(jax.ShapeDtypeStruct((local_expe...  85 us
    pallas_call x1, Pallas kernels, expert_ffn(): pl.pallas_call(ffn_kernel, out_shape=jax.ShapeDtypeStruct(x.shape, jnp.bf...  73.4 us

profile of v5, /device:TPU:0, one launch (start us, length us, event | category | flops | bytes accessed | tf_op | source)
XLA Modules:
  0.0 583.3 jit_solution(15274663161233591679)
XLA Ops:
  0.0 0.0 copy-start
  0.0 0.0 copy-start.1
  0.0 4.1 copy.18
  4.1 0.0 copy-done
  4.1 0.0 copy-done.1
  4.1 6.1 %copy_bitcast_fusion = (bf16[256,4096]{1,0:T(8,128)(2,1)}, bf16[256,4096]{1,0:T(8,128)(2,1)}) fusion(bf16[32,8,32,128]{3,2,1,0:T(8,128)(2,1)S(1)} %bitcast.35, bf16[32,8,32,128]{3,2,1,0:T(8,128)(2,1)S(1)} %bitcast.36), kind=kLoop, calls=%fused_computation | loop fusion | bytes 8388608 | tf_op jit(solution)/shard_map/reshape | solution.py:750
  10.2 244.1 %attend_heads.1 = (bf16[512,2048]{1,0:T(8,128)(2,1)}, bf16[512,2048]{1,0:T(8,128)(2,1)}, bf16[8,512,2048]{2,1,0:T(8,128)(2,1)}, f32[8,32,512]{2,1,0:T(8,128)}, s32[8,8,512]{2,1,0:T(8,128)}) custom-call(bf16[512,2048]{1,0:T(8,128)(2,1)} %bitcast.33, s32[8,512]{1,0:T(8,128)} %bitcast.37, bf16[256,4096]{1,0:T(8,128)(2,1)} %bitcast.31, ...), custom_call_target="tpu_custom_call" | custom-call | tf_op jit(solution)/shard_map/attend_heads/pallas_call | solution.py:330
  254.3 1.0 slice_reduce_fusion
  255.3 0.1 copy.11
  255.4 0.6 reshape.26.units_ref
  256.0 85.0 %spread_rows.1 = (bf16[16,8,64,2048]{3,2,1,0:T(8,128)(2,1)}, f32[8,8,512]{2,1,0:T(8,128)}) custom-call(bf16[512,2048]{1,0:T(8,128)(2,1)} %get-tuple-element.12.u_hbm, bf16[512,2048]{1,0:T(8,128)(2,1)} %get-tuple-element.13.h_ref.h_hbm, f32[2048,128]{1,0:T(8,128)} %router_ref.1, s32[8,512]{1,0:T(8,128)} %bitcast.38, ...), custom_call_target="tpu_custom_call" | custom-call | tf_op jit(solution)/shard_map/spread_rows/pallas_call | solution.py:476
  341.0 73.4 %expert_mlp.1.o_hbm = bf16[16,8,64,2048]{3,2,1,0:T(8,128)(2,1)} custom-call(s32[128]{0:T(128)} %reshape.26.units_ref, bf16[16,8,64,2048]{3,2,1,0:T(8,128)(2,1)} %get-tuple-element.14.x_ref, bf16[16,2048,768]{2,1,0:T(8,128)(2,1)} %w1_hbm.1, bf16[16,2048,768]{2,1,0:T(8,128)(2,1)} %w3_hbm.1, bf16[16,768,2048]{2,1,0:T(8,128)(2,1)} %w2_hbm.1), custom_call_target="tpu_custom_call" | custom-call | tf_op jit(solution)/shard_map/expert_mlp/pallas_call | solution.py:562
  414.4 165.7 %combine_rows.1 = bf16[512,2048]{1,0:T(8,128)(2,1)} custom-call(bf16[16,8,64,2048]{3,2,1,0:T(8,128)(2,1)} %expert_mlp.1.o_hbm, f32[8,32,512]{2,1,0:T(8,128)} %get-tuple-element.11.slot_ref.slots_ref, s32[8,8,512]{2,1,0:T(8,128)} %get-tuple-element.15.ids_ref, f32[8,8,512]{2,1,0:T(8,128)} %get-tuple-element.16.gates_ref, ...), custom_call_target="tpu_custom_call" | custom-call | tf_op jit(solution)/shard_map/combine_rows/pallas_call | solution.py:728
  580.1 3.2 copy.20
  (1 shorter events, 0.0 us)
Async XLA Ops:
  0.0 4.1 copy-start
  0.0 4.1 copy-start.1

commit v6 on v5

--- a/solution.py
+++ b/solution.py
@@ -625,6 +625,8 @@
         for j in range(ids_ref.shape[1]):
             gate = gate + jnp.where(ids_ref[target, j:j + 1, :] == wanted, gates_ref[target, j:j + 1, :], 0.0)
         gate_tab[...] = gate
+
+    def open_rows(i):
         own_copy(i).wait()
         to_mate(i).wait_recv()
 
@@ -653,6 +655,11 @@
             open_dest(i)
 
         weights(i, part)
+
+        @pl.when(part == 0)
+        def _():
+            open_rows(i)
+
         slot = lax.rem(i, CORES)
         depth = experts * CAP
 
@@ -686,8 +693,13 @@
     residual.wait()
 
     def phase_three(step, c):
+        products(6 + step // part_n, lax.rem(step, part_n), p_last.at[step])
+        return c
+
+    lax.fori_loop(0, pair_n, phase_three, 0)
+
+    def close(step, c):
         part = lax.rem(step, part_n)
-        products(6 + step // part_n, part, p_last.at[step])
         n = jnp.where(step < part_n, 1 - core, core) * part_n + part
         one_copy(pair_n + n).wait_recv()
         two_copy(n).wait_recv()
@@ -704,7 +716,7 @@
 
         return c
 
-    lax.fori_loop(0, pair_n, phase_three, 0)
+    lax.fori_loop(0, pair_n, close, 0)
     for n in range(part_n):
         rows = pl.ds(n * rows_n, rows_n)
         last_copy(n).wait_recv()

time: 581 us -> 572 us (0.985)
  Pallas kernels: 568 us -> 558 us
    pallas_call x1, Pallas kernels: 166 us -> 159 us  [combine(): pl.pallas_call(combine_kernel, out_shape=jax.ShapeDtypeStruct((tok, dim),...]
where the time goes in v6:
time: 572 us; the launch traced here: 573 us
  Pallas kernels  558 us (98%)
  local copies, waits for them, and re-layouts  14 us (2%)
    pallas_call x1, Pallas kernels, attend(): pl.pallas_call(attend_kernel, out_shape=(jax.ShapeDtypeStruct((tok, dim),...  244 us
    pallas_call x1, Pallas kernels, combine(): pl.pallas_call(combine_kernel, out_shape=jax.ShapeDtypeStruct((tok, dim),...  159 us
    pallas_call x1, Pallas kernels, spread(): pl.pallas_call(spread_kernel, out_shape=(jax.ShapeDtypeStruct((local_expe...  85 us
    pallas_call x1, Pallas kernels, expert_ffn(): pl.pallas_call(ffn_kernel, out_shape=jax.ShapeDtypeStruct(x.shape, jnp.bf...  69.9 us

profile of v6, /device:TPU:0, one launch (start us, length us, event | category | flops | bytes accessed | tf_op | source)
XLA Modules:
  0.0 573.0 jit_solution(8183831921041012345)
XLA Ops:
  0.0 0.0 copy-start
  0.0 0.0 copy-start.1
  0.0 4.1 copy.18
  4.1 0.0 copy-done
  4.1 0.0 copy-done.1
  4.1 6.1 %copy_bitcast_fusion = (bf16[256,4096]{1,0:T(8,128)(2,1)}, bf16[256,4096]{1,0:T(8,128)(2,1)}) fusion(bf16[32,8,32,128]{3,2,1,0:T(8,128)(2,1)S(1)} %bitcast.35, bf16[32,8,32,128]{3,2,1,0:T(8,128)(2,1)S(1)} %bitcast.36), kind=kLoop, calls=%fused_computation | loop fusion | bytes 8388608 | tf_op jit(solution)/shard_map/reshape | solution.py:762
  10.2 244.1 %attend_heads.1 = (bf16[512,2048]{1,0:T(8,128)(2,1)}, bf16[512,2048]{1,0:T(8,128)(2,1)}, bf16[8,512,2048]{2,1,0:T(8,128)(2,1)}, f32[8,32,512]{2,1,0:T(8,128)}, s32[8,8,512]{2,1,0:T(8,128)}) custom-call(bf16[512,2048]{1,0:T(8,128)(2,1)} %bitcast.33, s32[8,512]{1,0:T(8,128)} %bitcast.37, bf16[256,4096]{1,0:T(8,128)(2,1)} %bitcast.31, ...), custom_call_target="tpu_custom_call" | custom-call | tf_op jit(solution)/shard_map/attend_heads/pallas_call | solution.py:330
  254.3 1.0 slice_reduce_fusion
  255.3 0.1 copy.11
  255.4 0.6 reshape.26.units_ref
  256.0 85.0 %spread_rows.1 = (bf16[16,8,64,2048]{3,2,1,0:T(8,128)(2,1)}, f32[8,8,512]{2,1,0:T(8,128)}) custom-call(bf16[512,2048]{1,0:T(8,128)(2,1)} %get-tuple-element.12.u_hbm, bf16[512,2048]{1,0:T(8,128)(2,1)} %get-tuple-element.13.h_ref.h_hbm, f32[2048,128]{1,0:T(8,128)} %router_ref.1, s32[8,512]{1,0:T(8,128)} %bitcast.38, ...), custom_call_target="tpu_custom_call" | custom-call | tf_op jit(solution)/shard_map/spread_rows/pallas_call | solution.py:476
  341.0 69.9 %expert_mlp.1.o_hbm = bf16[16,8,64,2048]{3,2,1,0:T(8,128)(2,1)} custom-call(s32[128]{0:T(128)} %reshape.26.units_ref, bf16[16,8,64,2048]{3,2,1,0:T(8,128)(2,1)} %get-tuple-element.14.x_ref, bf16[16,2048,768]{2,1,0:T(8,128)(2,1)} %w1_hbm.1, bf16[16,2048,768]{2,1,0:T(8,128)(2,1)} %w3_hbm.1, bf16[16,768,2048]{2,1,0:T(8,128)(2,1)} %w2_hbm.1), custom_call_target="tpu_custom_call" | custom-call | tf_op jit(solution)/shard_map/expert_mlp/pallas_call | solution.py:562
  410.9 158.9 %combine_rows.1 = bf16[512,2048]{1,0:T(8,128)(2,1)} custom-call(bf16[16,8,64,2048]{3,2,1,0:T(8,128)(2,1)} %expert_mlp.1.o_hbm, f32[8,32,512]{2,1,0:T(8,128)} %get-tuple-element.11.slot_ref.slots_ref, s32[8,8,512]{2,1,0:T(8,128)} %get-tuple-element.15.ids_ref, f32[8,8,512]{2,1,0:T(8,128)} %get-tuple-element.16.gates_ref, ...), custom_call_target="tpu_custom_call" | custom-call | tf_op jit(solution)/shard_map/combine_rows/pallas_call | solution.py:740
  569.8 3.2 copy.20
  (1 shorter events, 0.0 us)
Async XLA Ops:
  0.0 4.1 copy-start
  0.0 4.1 copy-start.1

commit v7 on v6

--- a/solution.py
+++ b/solution.py
@@ -439,7 +439,7 @@
         for expert in range(local_experts):
             hit = slot_ref[source, expert:expert + 1, :] == spot
             hbuf[expert * CAP:(expert + 1) * CAP, :] = jnp.where(hit, 1.0, 0.0).astype(jnp.bfloat16)
-        width = 256
+        width = 4 * TILE
 
         def tile(n, c):
             cols = pl.ds(pl.multiple_of(n * width, width), width)
@@ -663,15 +663,17 @@
         slot = lax.rem(i, CORES)
         depth = experts * CAP
 
+        wide = CORES * TILE
+
         def tile(n, c):
-            cols = pl.ds(pl.multiple_of(n * TILE, TILE), TILE)
-            mine = own[slot, :, :, cols].reshape(depth, TILE)
-            other = mate_rows[i, :, :, cols].reshape(depth, TILE)
+            cols = pl.ds(pl.multiple_of(n * wide, wide), wide)
+            mine = own[slot, :, :, cols].reshape(depth, wide)
+            other = mate_rows[i, :, :, cols].reshape(depth, wide)
             out = jnp.dot(gate3[:, :depth], mine, preferred_element_type=jnp.float32) + jnp.dot(gate3[:, depth:], other, preferred_element_type=jnp.float32)
             sink[:, cols] = sum(out[rows] for rows in strips(out.shape[0], rows_n))
             return c
 
-        lax.fori_loop(0, half // TILE, tile, 0)
+        lax.fori_loop(0, half // wide, tile, 0)
 
     lead, pair_n, part_n = p_one.shape[0], p_two.shape[0], p_two.shape[0] // CORES
 

time: 572 us -> 568 us (level)
  no operation moved by 1% of the time
where the time goes in v7:
time: 568 us; the launch traced here: 569 us
  Pallas kernels  554 us (98%)
  local copies, waits for them, and re-layouts  14 us (2%)
    pallas_call x1, Pallas kernels, attend(): pl.pallas_call(attend_kernel, out_shape=(jax.ShapeDtypeStruct((tok, dim),...  244 us
    pallas_call x1, Pallas kernels, combine(): pl.pallas_call(combine_kernel, out_shape=jax.ShapeDtypeStruct((tok, dim),...  157 us
    pallas_call x1, Pallas kernels, spread(): pl.pallas_call(spread_kernel, out_shape=(jax.ShapeDtypeStruct((local_expe...  82.9 us
    pallas_call x1, Pallas kernels, expert_ffn(): pl.pallas_call(ffn_kernel, out_shape=jax.ShapeDtypeStruct(x.shape, jnp.bf...  70.5 us

profile of v7, /device:TPU:0, one launch (start us, length us, event | category | flops | bytes accessed | tf_op | source)
XLA Modules:
  0.0 569.4 jit_solution(14405623144053263920)
XLA Ops:
  0.0 0.0 copy-start
  0.0 0.0 copy-start.1
  0.0 4.1 copy.18
  4.1 0.0 copy-done
  4.1 0.0 copy-done.1
  4.1 6.1 %copy_bitcast_fusion = (bf16[256,4096]{1,0:T(8,128)(2,1)}, bf16[256,4096]{1,0:T(8,128)(2,1)}) fusion(bf16[32,8,32,128]{3,2,1,0:T(8,128)(2,1)S(1)} %bitcast.35, bf16[32,8,32,128]{3,2,1,0:T(8,128)(2,1)S(1)} %bitcast.36), kind=kLoop, calls=%fused_computation | loop fusion | bytes 8388608 | tf_op jit(solution)/shard_map/reshape | solution.py:764
  10.2 244.1 %attend_heads.1 = (bf16[512,2048]{1,0:T(8,128)(2,1)}, bf16[512,2048]{1,0:T(8,128)(2,1)}, bf16[8,512,2048]{2,1,0:T(8,128)(2,1)}, f32[8,32,512]{2,1,0:T(8,128)}, s32[8,8,512]{2,1,0:T(8,128)}) custom-call(bf16[512,2048]{1,0:T(8,128)(2,1)} %bitcast.33, s32[8,512]{1,0:T(8,128)} %bitcast.37, bf16[256,4096]{1,0:T(8,128)(2,1)} %bitcast.31, ...), custom_call_target="tpu_custom_call" | custom-call | tf_op jit(solution)/shard_map/attend_heads/pallas_call | solution.py:330
  254.3 1.0 slice_reduce_fusion
  255.3 0.1 copy.11
  255.4 0.6 reshape.26.units_ref
  256.0 82.9 %spread_rows.1 = (bf16[16,8,64,2048]{3,2,1,0:T(8,128)(2,1)}, f32[8,8,512]{2,1,0:T(8,128)}) custom-call(bf16[512,2048]{1,0:T(8,128)(2,1)} %get-tuple-element.12.u_hbm, bf16[512,2048]{1,0:T(8,128)(2,1)} %get-tuple-element.13.h_ref.h_hbm, f32[2048,128]{1,0:T(8,128)} %router_ref.1, s32[8,512]{1,0:T(8,128)} %bitcast.38, ...), custom_call_target="tpu_custom_call" | custom-call | tf_op jit(solution)/shard_map/spread_rows/pallas_call | solution.py:476
  338.9 70.5 %expert_mlp.1.o_hbm = bf16[16,8,64,2048]{3,2,1,0:T(8,128)(2,1)} custom-call(s32[128]{0:T(128)} %reshape.26.units_ref, bf16[16,8,64,2048]{3,2,1,0:T(8,128)(2,1)} %get-tuple-element.14.x_ref, bf16[16,2048,768]{2,1,0:T(8,128)(2,1)} %w1_hbm.1, bf16[16,2048,768]{2,1,0:T(8,128)(2,1)} %w3_hbm.1, bf16[16,768,2048]{2,1,0:T(8,128)(2,1)} %w2_hbm.1), custom_call_target="tpu_custom_call" | custom-call | tf_op jit(solution)/shard_map/expert_mlp/pallas_call | solution.py:562
  409.4 156.9 %combine_rows.1 = bf16[512,2048]{1,0:T(8,128)(2,1)} custom-call(bf16[16,8,64,2048]{3,2,1,0:T(8,128)(2,1)} %expert_mlp.1.o_hbm, f32[8,32,512]{2,1,0:T(8,128)} %get-tuple-element.11.slot_ref.slots_ref, s32[8,8,512]{2,1,0:T(8,128)} %get-tuple-element.15.ids_ref, f32[8,8,512]{2,1,0:T(8,128)} %get-tuple-element.16.gates_ref, ...), custom_call_target="tpu_custom_call" | custom-call | tf_op jit(solution)/shard_map/combine_rows/pallas_call | solution.py:742
  566.3 3.2 copy.20
  (1 shorter events, 0.0 us)
Async XLA Ops:
  0.0 4.1 copy-start
  0.0 4.1 copy-start.1
